TPU v7x, 32 devices: a whole 2x2x4 slice. The times are simulated.
32 devices in a mesh: shard: 4 (over y, x), rep: 8 (over z, core).
Axes of the slice: x: 2, y: 2, z: 4, core: 2. Of those that a mesh axis runs over, the one named last changes fastest.
Arguments:
- activations: bfloat16 [8, 512, 2048], P('rep', 'shard'), may hold values from -16 to 16
- segments: int32 [8, 512], P('rep'), may hold values from 0 to 3, never falling along the last dimension, each value on 1 to 256 neighbouring positions
- attn_gain: float32 [2048], replicated, may hold values from 0.25 to 1.75
- query_weight: bfloat16 [2048, 2048], P('shard'), may hold values from -0.125 to 0.125
- key_weight: bfloat16 [2048, 1024], P('shard'), may hold values from -0.125 to 0.125
- value_weight: bfloat16 [2048, 1024], P('shard'), may hold values from -0.125 to 0.125
- query_gain: float32 [128], replicated, may hold values from 0.5 to 5.5
- key_gain: float32 [128], replicated, may hold values from 0.5 to 5.5
- out_weight: bfloat16 [2048, 2048], P('shard'), may hold values from -0.75 to 0.75
- mlp_gain: float32 [2048], replicated, may hold values from 0.25 to 1.75
- gate_weight: bfloat16 [2048, 6144], P('shard'), may hold values from -0.125 to 0.125
- up_weight: bfloat16 [2048, 6144], P('shard'), may hold values from -0.125 to 0.125
- down_weight: bfloat16 [6144, 2048], P('shard'), may hold values from -0.078125 to 0.078125
- cotangent: bfloat16 [8, 512, 2048], P('rep', 'shard'), may hold values from -11.1 to 11.1
Outputs:
- output: bfloat16 [8, 512, 2048], P('rep', 'shard')
- grad_input: float32 [8, 512, 2048], P('rep', 'shard')
- grad_attn_gain: float32 [2048], replicated
- grad_query_weight: float32 [2048, 2048], P('shard')
- grad_key_weight: float32 [2048, 1024], P('shard')
- grad_value_weight: float32 [2048, 1024], P('shard')
- grad_query_gain: float32 [128], replicated
- grad_key_gain: float32 [128], replicated
- grad_out_weight: float32 [2048, 2048], P('shard')
- grad_mlp_gain: float32 [2048], replicated
- grad_gate_weight: float32 [2048, 6144], P('shard')
- grad_up_weight: float32 [2048, 6144], P('shard')
- grad_down_weight: float32 [6144, 2048], P('shard')
Inputs may be any that keep to these rules, and one draw needn't show every extreme that they name: `segments`: within each sequence the document numbers never fall; each document has 1 to 256 tokens, and one has exactly 256.
All inputs are finite; a program needn't handle non-finite values.
Results may differ from a plain program's by a relative error of at most 0.02.
The roundings to bfloat16 on the way count: a program that leaves them out, or rounds other values in their place, can miss the bound.
Values may be sent and summed in bfloat16 or wider, within the bound.
A program may use at most 384 MiB of HBM per device.

v0:
```python
from functools import partial
import math

import jax
import jax.numpy as jnp
from jax import lax
from jax.experimental import pallas as pl
from jax.experimental.pallas import tpu as pltpu
from jax.sharding import PartitionSpec as P

HQ = 16
HK = 8
HD = 128
FF = 6144
GROUPS = HQ // HK

EPSILON = 1e-06
ROPE_BASE = 1000000.0
MASKED = -1e30
BF = jnp.bfloat16
F32 = jnp.float32

HOOK_TICKS = (0, 4, 6, 7, 8, 9, 11, 12, 13, 14, 15, 16, 18)


def dot(a, b):
    return jnp.dot(a, b, preferred_element_type=F32)


def dot_last(a, b):
    return lax.dot_general(a, b, (((1,), (1,)), ((), ())), preferred_element_type=F32)


def dot_first(a, b):
    return lax.dot_general(a, b, (((0,), (0,)), ((), ())), preferred_element_type=F32)


def positions(seg_ids):
    token_index = jnp.arange(seg_ids.shape[0], dtype=jnp.int32)
    before = jnp.concatenate([jnp.full((1,), -1, jnp.int32), seg_ids[:-1]])
    starts = lax.cummax(
        jnp.where(seg_ids != before, token_index, jnp.zeros_like(token_index)), axis=0
    )
    return (token_index - starts).astype(F32)


def head_rope(raw, gain, cos2, sin2):
    rstat = lax.rsqrt(jnp.mean(raw * raw, -1, keepdims=True) + EPSILON)
    scaled = raw * rstat * gain
    return scaled * cos2 + pltpu.roll(scaled, HD // 2, 1) * sin2


def attend_pair(qkv, j, nq, nk, qg, kg, cos2, sin2, trow, tcol, o_ref, qr_ref, kr_ref, vb_ref, scale):
    length = qkv.shape[0]
    block = min(length, 512)
    own = slice(j * HD, (j + 1) * HD)
    at = (nq + j) * HD
    kr = head_rope(qkv[:, at : at + HD], kg[...], cos2[...], sin2[...]).astype(BF)
    at = (nq + nk + j) * HD
    vb = qkv[:, at : at + HD].astype(BF)
    kr_ref[:, own] = kr
    vb_ref[:, own] = vb
    for g in range(GROUPS):
        cols = slice((j * GROUPS + g) * HD, (j * GROUPS + g + 1) * HD)
        qr_ref[:, cols] = head_rope(qkv[:, cols], qg[...], cos2[...], sin2[...]).astype(BF)
        for b in range(length // block):
            rows = slice(b * block, (b + 1) * block)
            s = dot_last(qr_ref[rows, cols], kr) * scale
            seen = (tcol[0:1, :] <= trow[rows, 0:1]) & (tcol[1:2, :] == trow[rows, 1:2])
            s = jnp.where(seen, s, MASKED)
            e = jnp.exp(s - jnp.max(s, -1, keepdims=True))
            p = (e / jnp.sum(e, -1, keepdims=True)).astype(BF)
            o_ref[rows, cols] = dot(p, vb).astype(BF)


def head_back(grad_rot, raw, gain, cos2, sin2):
    back = grad_rot * cos2 - pltpu.roll(grad_rot, HD // 2, 1) * sin2
    rstat = lax.rsqrt(jnp.mean(raw * raw, -1, keepdims=True) + EPSILON)
    scaled = raw * rstat
    gain_part = jnp.sum(back * scaled, 0, keepdims=True)
    b = back * gain
    return rstat * (b - scaled * jnp.mean(b * scaled, -1, keepdims=True)), gain_part


def attend_back_pair(
    j, nq, nk, qkv, qr_ref, kr_ref, vb_ref, do_ref, dqkv, qg, kg, cos_ref, sin_ref, trow, tcol, scale
):
    cos2, sin2 = cos_ref[...], sin_ref[...]
    own = slice(j * HD, (j + 1) * HD)
    length = qkv.shape[0]
    block = min(length, 256)
    kr, vb = kr_ref[:, own], vb_ref[:, own]
    dkr = jnp.zeros((length, HD), F32)
    dv = jnp.zeros((length, HD), F32)
    gq = jnp.zeros((1, HD), F32)
    for g in range(GROUPS):
        cols = slice((j * GROUPS + g) * HD, (j * GROUPS + g + 1) * HD)
        dqr = []
        for b in range(length // block):
            rows = slice(b * block, (b + 1) * block)
            qr, do = qr_ref[rows, cols], do_ref[rows, cols]
            s = dot_last(qr, kr) * scale
            seen = (tcol[0:1, :] <= trow[rows, 0:1]) & (tcol[1:2, :] == trow[rows, 1:2])
            s = jnp.where(seen, s, MASKED)
            e = jnp.exp(s - jnp.max(s, -1, keepdims=True))
            p = e / jnp.sum(e, -1, keepdims=True)
            dp = dot_last(do, vb)
            ds = (p * (dp - jnp.sum(p * dp, -1, keepdims=True))).astype(BF)
            dqr.append(dot(ds, kr) * scale)
            dkr += dot_first(ds, qr)
            dv += dot_first(p.astype(BF), do)
        dqr = dqr[0] if len(dqr) == 1 else jnp.concatenate(dqr, 0)
        dq, part = head_back(dqr, qkv[:, cols], qg[...], cos2, sin2)
        dqkv[:, cols] = dq.astype(BF)
        gq += part
    at = (nq + j) * HD
    dk, gk = head_back(dkr * scale, qkv[:, at : at + HD], kg[...], cos2, sin2)
    dqkv[:, at : at + HD] = dk.astype(BF)
    at = (nq + nk + j) * HD
    dqkv[:, at : at + HD] = dv.astype(BF)
    return gq, gk


def assemble_kernel(counts, order_ref, *refs):
    n_rows, n_cols = counts
    total = n_rows + n_cols
    mine, other, outs = refs[:total], refs[total : 2 * total], refs[2 * total :]

    def fill(sources):
        for src, out in zip(sources, outs):
            m, places, q, width = src.shape
            for a in range(places):
                out[a * m * q : (a + 1) * m * q, :] = (
                    src[:, a].reshape(m * q, width).astype(F32)
                )

    pl.when(pl.program_id(0) == 0)(lambda: fill(mine))
    pl.when(pl.program_id(0) == 1)(lambda: fill(other))


def assemble(rows, cols, core, owner):
    n = len(owner)
    order = jnp.stack(list(owner) + [core]).astype(jnp.int32)
    in_specs, out_specs, shapes, operands = [[], []], [], [], [[], []]
    size = 0
    for mine, other in rows:
        m, places, q, width = mine.shape
        block = (m, places, q, width // n)
        in_specs[0].append(
            pl.BlockSpec(block, lambda g, b, o: (0, 0, 0, jnp.where(g == 0, b, n - 1)))
        )
        in_specs[1].append(
            pl.BlockSpec(block, lambda g, b, o: (0, 0, 0, jnp.where(g == 0, 0, b)))
        )
        out_specs.append(
            pl.BlockSpec((places * m * q, width // n), lambda g, b, o: (g ^ o[n], b))
        )
        shapes.append(jax.ShapeDtypeStruct((2 * places * m * q, width), F32))
        operands[0].append(mine)
        operands[1].append(other)
        size += mine.size
    for mine, other, at, width in cols:
        m, _, q, _ = mine.shape
        block = (m, 1, q, width)
        in_specs[0].append(
            pl.BlockSpec(block, lambda g, b, o, at=at: (0, o[jnp.where(g == 0, b, n - 1)], 0, at))
        )
        in_specs[1].append(
            pl.BlockSpec(block, lambda g, b, o, at=at: (0, o[jnp.where(g == 0, 0, b)], 0, at))
        )
        out_specs.append(pl.BlockSpec((m * q, width), lambda g, b, o: (g ^ o[n], b)))
        shapes.append(jax.ShapeDtypeStruct((2 * m * q, n * width), F32))
        operands[0].append(mine)
        operands[1].append(other)
        size += m * n * q * width
    return pl.pallas_call(
        partial(assemble_kernel, (len(rows), len(cols))),
        out_shape=tuple(shapes),
        grid_spec=pltpu.PrefetchScalarGridSpec(
            num_scalar_prefetch=1,
            grid=(2, n),
            in_specs=in_specs[0] + in_specs[1],
            out_specs=tuple(out_specs),
        ),
        compiler_params=pltpu.CompilerParams(vmem_limit_bytes=56 << 20),
        cost_estimate=pl.CostEstimate(flops=0, bytes_accessed=12 * size, transcendentals=0),
        name="assemble",
    )(order, *operands[0], *operands[1])


MESH_ID = pl.DeviceIdType.MESH


def back_kernel(n, m, nq, nk, scale, parts, *refs):
    (x_hbm, hidden_hbm, wo_hbm, wd_hbm, qkv_mine, qkv_other, mlp_mine, mlp_other,
     qkv_hbm, qr_hbm, kr_hbm, vb_hbm, o_hbm, normed_hbm, hn_hbm, act_hbm, dy_hbm, dpre_hbm,
     ag, mg, qg, kg, cos2, sin2, trow, tcol,
     output, grad_in, gain_out) = refs[:29]
    mines, others, away_v, fins, refs = refs[29:33], refs[33:37], refs[37:41], refs[41:45], refs[45:]
    (ups, downs, send_v,
     x_v, hidden, wo, qkv, qr, kr, vb, o, normed, hn, act, dy_all, dpre,
     part_s, part_r, out_r, dz_all, do, dqkv, wtile, dtile, gain_ref,
     pair_s, pair_r, up_s, up_r, down_s, down_r,
     peer_s, peer_r, gup_s, gup_r, gdown_s, gdown_r, sib_s, sib_r, own_sem, gain_pair, gain_group,
     gain_line, gain_s, gain_r, in_sem, wt_sem, dhn_s, dhn_r, dz_s, dz_r, dn_s, dn_r, out_ss,
     out_rs) = refs
    rows, width = x_v.shape
    own = width // n
    half = own // 2
    ring = ups.shape[0]
    shard, rep = lax.axis_index("shard"), lax.axis_index("rep")
    i = rep // 2
    core = lax.rem(rep, 2)
    sibling = {"rep": 2 * i + 1 - core}
    above, below = {"rep": rep + 2}, {"rep": rep - 2}
    peers = [None] + [{"shard": shard ^ k} for k in range(1, n)]
    has_up, has_down = i < m - 1, i > 0

    barrier = pltpu.get_barrier_semaphore()

    def greet(dev):
        pl.semaphore_signal(barrier, inc=1, device_id=dev, device_id_type=MESH_ID)

    greet(sibling)
    for k in range(1, n):
        greet(peers[k])
    line = [None] + [{"rep": 2 * lax.rem(i + d, m) + core} for d in range(1, m)]
    for d in range(1, m):
        greet(line[d])

    loads = [
        pltpu.make_async_copy(src, dst, in_sem.at[f])
        for f, (src, dst) in enumerate(
            [
                (act_hbm, act), (dy_hbm, dy_all), (dpre_hbm, dpre), (hn_hbm, hn),
                (hidden_hbm, hidden), (wo_hbm, wo), (qkv_hbm, qkv), (qr_hbm, qr), (kr_hbm, kr),
                (vb_hbm, vb), (o_hbm, o), (normed_hbm, normed), (x_hbm, x_v),
            ]
        )
    ]
    for copy in loads:
        copy.start()
    pl.semaphore_wait(barrier, n + m - 1)

    def remote(src, dst, ssem, rsem, dev):
        return pltpu.make_async_remote_copy(
            src_ref=src, dst_ref=dst, send_sem=ssem, recv_sem=rsem,
            device_id=dev, device_id_type=MESH_ID,
        )

    def cols_of(p):
        return pl.ds(parts[p][3], parts[p][4])

    def chunk(p, j):
        seg, at = parts[p][:2]
        return away_v[seg].at[at, j, :, cols_of(p)]

    def fin(p):
        seg, at = parts[p][:2]
        return fins[seg].at[at, :, cols_of(p)]

    def out(refs, p, j):
        seg, at = parts[p][:2]
        return refs[seg].at[j, at, :, cols_of(p)]

    def pair_copy(p):
        seg, at = parts[p][:2]
        return remote(
            send_v.at[p % 3, :, :, pl.ds(0, parts[p][4])], away_v[seg].at[at, :, :, cols_of(p)],
            pair_s.at[p], pair_r.at[p], sibling,
        )

    def slot(ref, p, t):
        return ref.at[p % ring, t, :, pl.ds(0, parts[p][4])]

    def up_copy(p, t, src):
        return remote(src, slot(ups, p, t), up_s.at[p, t], up_r.at[p, t], above)

    def down_copy(p, t, src):
        return remote(src, slot(downs, p, t), down_s.at[p, t], down_r.at[p, t], below)

    def add_into(ref, other):
        ref[...] = (ref[...].astype(F32) + other[...].astype(F32)).astype(BF)

    def scatter_step(p, t):
        if t > 0:

            @pl.when((i > 0) & (i <= t) & has_up)
            def _():
                up_copy(p, t - 1, slot(ups, p, t - 1)).wait_recv()
                add_into(slot(ups, p, t - 1), chunk(p, m - 1 - t + i))

            @pl.when((i < m - 1) & (i >= m - 1 - t) & has_down)
            def _():
                down_copy(p, t - 1, slot(downs, p, t - 1)).wait_recv()
                add_into(slot(downs, p, t - 1), chunk(p, i - (m - 1 - t)))

            pl.when((i > 0) & (i <= t) & has_up)(
                lambda: up_copy(p, t, slot(ups, p, t - 1)).start()
            )
            pl.when((i < m - 1) & (i >= m - 1 - t) & has_down)(
                lambda: down_copy(p, t, slot(downs, p, t - 1)).start()
            )
        pl.when(i == 0)(lambda: up_copy(p, t, chunk(p, m - 1 - t)).start())
        pl.when(i == m - 1)(lambda: down_copy(p, t, chunk(p, t)).start())

    def peer_copy(p):
        return remote(chunk(p, i), fin(p), peer_s.at[p], peer_r.at[p], peers[parts[p][2]])

    def total(p):
        pl.when(has_down)(lambda: up_copy(p, m - 2, slot(ups, p, m - 2)).wait_recv())
        pl.when(has_up)(lambda: down_copy(p, m - 2, slot(downs, p, m - 2)).wait_recv())
        where = fin(p) if parts[p][2] == 0 else chunk(p, i)

        def put(*extra):
            value = chunk(p, i)[...].astype(F32)
            for e in extra:
                value = value + e[...].astype(F32)
            where[...] = value.astype(BF)

        u, d = slot(ups, p, m - 2), slot(downs, p, m - 2)
        pl.when(has_up & has_down)(lambda: put(u, d))
        pl.when(has_up & (i == 0))(lambda: put(d))
        pl.when(has_down & (i == m - 1))(lambda: put(u))
        if parts[p][2] != 0:
            peer_copy(p).start()

    def gup_copy(p, t, j, src):
        return remote(src, out(mines, p, j), gup_s.at[p, t], gup_r.at[p, t], above)

    def gdown_copy(p, t, j, src):
        return remote(src, out(mines, p, j), gdown_s.at[p, t], gdown_r.at[p, t], below)

    def sib_copy(p, j, src):
        return remote(src, out(others, p, j), sib_s.at[p, j], sib_r.at[p, j], sibling)

    def own_copy(p):
        return pltpu.make_async_copy(fin(p), out(mines, p, i), own_sem.at[p])

    def gather_step(p, t):
        if t == 0:
            for u in range(m - 1):
                pl.when((i <= u) & has_up)(lambda: up_copy(p, u, slot(ups, p, u)).wait_send())
                pl.when((i >= m - 1 - u) & has_down)(
                    lambda: down_copy(p, u, slot(downs, p, u)).wait_send()
                )
            if parts[p][2] != 0:
                peer_copy(p).wait_recv()
            pl.when(has_up)(lambda: gup_copy(p, 0, i, fin(p)).start())
            pl.when(has_down)(lambda: gdown_copy(p, 0, i, fin(p)).start())
            sib_copy(p, i, fin(p)).start()
            own_copy(p).start()
            return

        @pl.when(i - t >= 0)
        def _():
            here = out(mines, p, i - t)
            gup_copy(p, t - 1, i - t, here).wait_recv()
            if t < m - 1:
                pl.when(has_up)(lambda: gup_copy(p, t, i - t, here).start())
            sib_copy(p, i - t, here).start()

        @pl.when(i + t < m)
        def _():
            here = out(mines, p, i + t)
            gdown_copy(p, t - 1, i + t, here).wait_recv()
            if t < m - 1:
                pl.when(has_down)(lambda: gdown_copy(p, t, i + t, here).start())
            sib_copy(p, i + t, here).start()

    def gain_copies(level):
        if level == 0:
            return [remote(gain_ref, gain_pair, gain_s.at[0], gain_r.at[0], sibling)]
        if level == 1:
            return [
                remote(
                    gain_group.at[shard], gain_group.at[shard], gain_s.at[k], gain_r.at[k], peers[k]
                )
                for k in range(1, n)
            ]
        return [
            remote(
                gain_line.at[i], gain_line.at[i], gain_s.at[n - 1 + d], gain_r.at[n - 1 + d], line[d]
            )
            for d in range(1, m)
        ]

    def gains(level):
        if level > 0:
            for copy in gain_copies(level - 1):
                copy.wait_recv()
        if level == 1:
            gain_group[shard] = gain_ref[...] + gain_pair[...]
        elif level == 2:
            value = gain_group[0]
            for k in range(1, n):
                value = value + gain_group[k]
            gain_line[i] = value
        elif level == 3:
            value = gain_line[0]
            for k in range(1, m):
                value = value + gain_line[k]
            gain_out[...] = value
        if level < 3:
            for copy in gain_copies(level):
                copy.start()

    def tiles(cols, first=0):
        step = max(v for v in range(HD, 513, HD) if cols % v == 0)
        return [(c, pl.ds(first + c, step), pl.ds(c, step)) for c in range(0, cols, step)]

    def product(p, h, at):
        seg, place, k = parts[p][:3]
        if seg in (0, 2):
            ref = act if seg == 0 else o
            both = ref.shape[1] // 2
            start = (core if h == 0 else 1 - core) * both + place * half
            left = ref[:, pl.ds(pl.multiple_of(start, half), half)]
            right = (dy_all if seg == 0 else dz_all)[:, :, at].reshape(n * rows, at.size)
        else:
            left = (hn if seg == 1 else normed)[:, (h * n + k) * half : (h * n + k + 1) * half]
            right = (dpre if seg == 1 else dqkv)[:, at]
        return dot_first(left, right).reshape(m, half // m, at.size)

    def send(p):
        if p >= 3:
            pair_copy(p - 3).wait_send()
        for _, at, to in tiles(parts[p][4], parts[p][3]):
            send_v[p % 3, :, :, to] = product(p, 1, at).astype(BF)
        pair_copy(p).start()

    def first(p):
        seg, place = parts[p][:2]
        pair_copy(p).wait_recv()
        for _, at, _ in tiles(parts[p][4], parts[p][3]):
            away_v[seg][place, :, :, at] = (
                product(p, 0, at) + away_v[seg][place, :, :, at].astype(F32)
            ).astype(BF)
        scatter_step(p, 0)

    def dhn_copy(k):
        return remote(part_s.at[k], part_r.at[k - 1], dhn_s.at[k], dhn_r.at[k], peers[k])

    def dn_copy(k):
        return remote(part_s.at[k], part_r.at[k - 1], dn_s.at[k], dn_r.at[k], peers[k])

    def out_copy(k):
        return remote(part_s.at[k], out_r.at[k - 1], out_ss.at[k], out_rs.at[k], peers[k])

    def dz_copy(k):
        return remote(dz_all.at[0], dz_all.at[k], dz_s.at[k], dz_r.at[k], peers[k])

    strip = min(rows, 32)

    def strips(body):
        pl.loop(0, rows // strip)(
            lambda b: body(pl.ds(pl.multiple_of(b * strip, strip), strip))
        )

    def add_gain(at, value):
        for b in range(value.shape[1] // HD):
            gain_ref[at + b : at + b + 1, :] += value[:, b * HD : (b + 1) * HD]

    def norm_back(values, gain, at, result):
        def body(r):
            v = values[r, :].astype(F32)
            rstat = lax.rsqrt(jnp.mean(v * v, -1, keepdims=True) + EPSILON)
            scaled = v * rstat
            grad = part_s[0, r, :].astype(F32)
            for k in range(1, n):
                grad = grad + part_r[k - 1, r, :].astype(F32)
            add_gain(at, jnp.sum(grad * scaled, 0, keepdims=True))
            weighted = grad * gain[...]
            result(
                r, rstat * (weighted - scaled * jnp.mean(weighted * scaled, -1, keepdims=True))
            )

        strips(body)

    def partial_rows(grads, mine, other):
        cols = grads.shape[1]

        def tile_copy(b):
            src = (mine if b < n else other).at[b % n]
            return pltpu.make_async_copy(
                src, wtile.at[b % 2, :, :, pl.ds(0, cols)], wt_sem.at[b % 2]
            )

        tile_copy(0).start()
        for b in range(2 * n):
            tile_copy(b).wait()
            if b + 1 < 2 * n:
                tile_copy(b + 1).start()
            h, kk = b // n, b % n
            at = pl.ds(
                pl.multiple_of((shard ^ kk) * own + (core if h == 0 else 1 - core) * half, half),
                half,
            )
            w = wtile[b % 2, :, :, :cols].reshape(half, cols)
            for k in range(n):
                part_s[k, :, at] = dot_last(grads[k * rows : (k + 1) * rows, :], w).astype(BF)

    def hook_dhn():
        loads[2].wait()
        partial_rows(dpre, mlp_mine, mlp_other)
        for k in range(1, n):
            dhn_copy(k).start()

    def hook_hidden():
        loads[4].wait()
        for k in range(1, n):
            dhn_copy(k).wait_recv()
        gain_ref[...] = jnp.zeros_like(gain_ref)

        def result(r, value):
            value = dy_all[0, r, :].astype(F32) + value
            grad_in[r, :] = value
            dz_all[0, r, :] = value.astype(BF)

        norm_back(hidden, mg, width // HD, result)
        for k in range(1, n):
            dz_copy(k).start()

    def hook_do():
        for copy in loads[5:]:
            copy.wait()
        for k in range(n):
            if k > 0:
                dz_copy(k).wait_recv()
            do[k * rows : (k + 1) * rows, :] = dot_last(dz_all[k], wo[...]).astype(BF)

    def hook_head(j):
        gq, gk = attend_back_pair(
            j, nq, nk, qkv, qr, kr, vb, do, dqkv, qg, kg, cos2, sin2, trow, tcol, scale
        )
        add_gain(2 * width // HD, gq)
        add_gain(2 * width // HD + 1, gk)

    def hook_normed():
        for k in range(1, n):
            dhn_copy(k).wait_send()
        partial_rows(dqkv, qkv_mine, qkv_other)
        for k in range(1, n):
            dn_copy(k).start()

    def hook_input():
        for k in range(1, n):
            dn_copy(k).wait_recv()

        def result(r, value):
            grad_in[r, :] = grad_in[r, :] + value

        norm_back(x_v, ag, 0, result)

    def hook_down():
        for k in range(1, n):
            dn_copy(k).wait_send()
        step = dtile.shape[2]

        def tile_copy(b):
            return pltpu.make_async_copy(
                wd_hbm.at[:, pl.ds(b * step, step)], dtile.at[b % 2], wt_sem.at[b % 2]
            )

        tile_copy(0).start()
        for b in range(width // step):
            tile_copy(b).wait()
            if b + 1 < width // step:
                tile_copy(b + 1).start()
            for k in range(n):
                part_s[k, :, b * step : (b + 1) * step] = dot(
                    act[k * rows : (k + 1) * rows, :], dtile[b % 2]
                ).astype(BF)
        for k in range(1, n):
            out_copy(k).start()

    def hook_output():
        for k in range(1, n):
            out_copy(k).wait_recv()

        def body(r):
            value = hidden[r, :] + part_s[0, r, :].astype(F32)
            for k in range(1, n):
                value = value + out_r[k - 1, r, :].astype(F32)
            output[r, :] = value.astype(BF)

        strips(body)

    at_tick = {}
    hooks = [hook_dhn, hook_hidden, hook_do] + [partial(hook_head, j) for j in range(nk)]
    hooks += [hook_normed, hook_input] + [partial(gains, level) for level in range(4)]
    hooks += [hook_down, hook_output]
    for hook, tick in zip(hooks, HOOK_TICKS[:3] + HOOK_TICKS[3 : 3 + nk] + HOOK_TICKS[-8:]):
        at_tick.setdefault(tick, []).append(hook)

    stages = [first] + [lambda p, t=t: scatter_step(p, t) for t in range(1, m - 1)]
    stages += [total] + [lambda p, t=t: gather_step(p, t) for t in range(m)]

    loads[0].wait()
    loads[1].wait()
    send(0)
    send(1)
    ticks = len(parts) + len(stages) - 1
    for tick in range(max(ticks, max(at_tick) + 1)):
        if tick == 0:
            loads[3].wait()
        for st in range(len(stages) - 1, -1, -1):
            p = tick - st
            if 0 <= p < len(parts):
                stages[st](p)
        for hook in at_tick.get(tick, []):
            hook()
        if tick + 2 < len(parts):
            send(tick + 2)

    for k in range(1, n):
        dz_copy(k).wait_send()
        out_copy(k).wait_send()
    for level in range(3):
        for copy in gain_copies(level):
            copy.wait_send()
    for p in range(len(parts)):
        if p >= len(parts) - 3:
            pair_copy(p).wait_send()
        if parts[p][2] != 0:
            peer_copy(p).wait_send()
        own_copy(p).wait()
        for t in range(m - 1):
            pl.when((i - t >= 0) & has_up)(lambda: gup_copy(p, t, i, fin(p)).wait_send())
            pl.when((i + t < m) & has_down)(lambda: gdown_copy(p, t, i, fin(p)).wait_send())
        for j in range(m):
            copy = sib_copy(p, j, fin(p))
            copy.wait_send()
            copy.wait_recv()


def back(n, m, nq, nk, x, hidden, wo, wd, weights, qkv, heads, o, normed, hn, act, dy_all, dpre,
         gains, tables):
    rows, width = x.shape
    length = n * rows
    q, cols = weights[0].shape[2:]
    wide = dpre.shape[1]
    half = m * q
    dma = pltpu.SemaphoreType.DMA
    sd = jax.ShapeDtypeStruct
    hbm, vmem = pl.BlockSpec(memory_space=pl.ANY), pl.BlockSpec(memory_space=pltpu.VMEM)
    segments = [
        (act.shape[1] // 2 // half, m, q, width), (n, m, q, wide),
        (nq * HD // 2 // half, m, q, width), (n, m, q, cols),
    ]

    def cut(seg, at, k, sizes):
        out, c = [], 0
        for size in sizes:
            out.append((seg, at, k, c, size))
            c += size
        return out

    parts = cut(0, 0, 0, [width // 4, width // 4, width // 2])
    for a in range(1, segments[0][0]):
        parts += cut(0, a, 0, [width // 2] * 2)
    for k in range(n):
        parts += cut(1, k, k, [wide // 2] * 2)
    for a in range(segments[2][0]):
        parts += cut(2, a, 0, [width // 2] * 2)
    for k in range(n):
        parts += cut(3, k, k, [cols] if k < n - 1 else [cols // 2] * 2)
    total = len(parts)
    most = max(part[4] for part in parts)
    ring = m + 2
    count = 2 * width // HD + 2
    gain_shape = (count + -count % 8, HD)
    outs = [sd((m, v[0]) + v[2:], BF) for v in segments]
    like = lambda v: pltpu.VMEM(v.shape, v.dtype)
    operands = [x, hidden, wo, wd, *weights, qkv, *heads, o, normed, hn, act, dy_all, dpre]
    return pl.pallas_call(
        partial(back_kernel, n, m, nq, nk, 1.0 / math.sqrt(HD), parts),
        out_shape=tuple(
            [sd((rows, width), BF), sd((rows, width), F32), sd(gain_shape, F32)] + outs + outs
        ),
        in_specs=[hbm] * len(operands) + [vmem] * 8,
        out_specs=tuple([vmem] * 3 + [hbm] * 8),
        scratch_shapes=[pltpu.VMEM(v, BF) for v in segments]
        + [pltpu.VMEM(v[:1] + v[2:], BF) for v in segments]
        + [pltpu.VMEM((ring, m - 1, q, most), BF)] * 2
        + [pltpu.VMEM((3, m, q, most), BF)]
        + [like(v) for v in (x, hidden, wo, qkv, *heads, o, normed, hn, act, dy_all, dpre)]
        + [
            pltpu.VMEM((n, rows, width), BF), pltpu.VMEM((n - 1, rows, width), BF),
            pltpu.VMEM((n - 1, rows, width), BF), pltpu.VMEM((n, rows, width), BF),
            pltpu.VMEM((length, nq * HD), BF), pltpu.VMEM((length, cols), BF),
            pltpu.VMEM((2, m, q, wide), BF), pltpu.VMEM((2, wd.shape[0], 256), BF),
            pltpu.VMEM(gain_shape, F32),
            dma((total,)), dma((total,)),
            dma((total, m - 1)), dma((total, m - 1)), dma((total, m - 1)), dma((total, m - 1)),
            dma((total,)), dma((total,)),
            dma((total, m - 1)), dma((total, m - 1)), dma((total, m - 1)), dma((total, m - 1)),
            dma((total, m)), dma((total, m)), dma((total,)),
            pltpu.VMEM(gain_shape, F32), pltpu.VMEM((n,) + gain_shape, F32),
            pltpu.VMEM((m,) + gain_shape, F32), dma((n + m,)), dma((n + m,)),
            dma((13,)), dma((2,)),
        ]
        + [dma((n,))] * 8,
        compiler_params=pltpu.CompilerParams(
            collective_id=3, has_side_effects=True, vmem_limit_bytes=67043328
        ),
        name="back",
    )(*operands, *gains, *tables)


def front_kernel(
    n, m, nq, nk, scale,
    x_hbm, dy_hbm, wq, wk, wv, wg, wu, wo_hbm,
    ag, qg, kg, mg, cos2, sin2, trow, tcol,
    normed, qkv, qr, kr, vb, o, hidden, hn, qkv_mine, qkv_other, mlp_mine, mlp_other, dy_all,
    x_all, wo, bounce, dy_v, hn_all, part_own, part_s, part_r,
    x_ss, x_rs, w_ss, w_rs, up_ss, up_rs, down_ss, down_rs, sib_ss, sib_rs,
    own_sem, back_sem, load_sem, part_ss, part_rs, hn_ss, hn_rs, dy_ss, dy_rs
):
    shard, rep = lax.axis_index("shard"), lax.axis_index("rep")
    i = rep // 2
    core = lax.rem(rep, 2)
    sibling = {"rep": 2 * i + 1 - core}
    above, below = {"rep": rep + 2}, {"rep": rep - 2}
    peers = [None] + [{"shard": shard ^ k} for k in range(1, n)]
    has_up, has_down = i < m - 1, i > 0
    rows, width = x_all.shape[1], x_all.shape[2]
    own = width // n
    half = own // 2

    barrier = pltpu.get_barrier_semaphore()

    def greet(dev):
        pl.semaphore_signal(barrier, inc=1, device_id=dev, device_id_type=MESH_ID)

    greet(sibling)
    for k in range(1, n):
        greet(peers[k])
    for d in range(1, m):
        greet({"rep": 2 * lax.rem(i + d, m) + core})
    pl.semaphore_wait(barrier, n + m - 1)

    def remote(src, dst, ssem, rsem, dev):
        return pltpu.make_async_remote_copy(
            src_ref=src, dst_ref=dst, send_sem=ssem, recv_sem=rsem,
            device_id=dev, device_id_type=MESH_ID,
        )

    groups = [
        ([wq, wk, wv], qkv_mine, qkv_other),
        ([wg, wu], mlp_mine, mlp_other),
    ]

    def fields(weights):
        at = 0
        for w in weights:
            size = w.shape[3] // n
            yield w, at, size
            at += size

    def cols_of(k, size):
        return pl.ds(pl.multiple_of((shard ^ k) * size, size), size)

    def piece_copies(g, k):
        weights, mine, _ = groups[g]
        return [
            remote(
                w.at[core, i, :, cols_of(k, size)],
                mine.at[k, i, :, pl.ds(at, size)],
                w_ss.at[g, k, f], w_rs.at[g, k, f], peers[k],
            )
            for f, (w, at, size) in enumerate(fields(weights))
        ]

    def own_copies(g):
        weights, mine, other = groups[g]
        out = []
        for h, dst in enumerate((mine, other)):
            for f, (w, at, size) in enumerate(fields(weights)):
                to = dst.at[0, :, :, pl.ds(at, size)] if g == 0 else bounce.at[h, :, :, pl.ds(at, size)]
                src = w.at[core if h == 0 else 1 - core, :, :, cols_of(0, size)]
                out.append(pltpu.make_async_copy(src, to, own_sem.at[g, h, f]))
        return out

    def back_copies():
        return [
            pltpu.make_async_copy(bounce.at[h], dst.at[0], back_sem.at[h])
            for h, dst in enumerate((mlp_mine, mlp_other))
        ]

    def region(ref, j):
        return ref.at[pl.ds(1, n - 1), j]

    def up_copy(g, t, j):
        r = region(groups[g][1], j)
        return remote(r, r, up_ss.at[g, t], up_rs.at[g, t], above)

    def down_copy(g, t, j):
        r = region(groups[g][1], j)
        return remote(r, r, down_ss.at[g, t], down_rs.at[g, t], below)

    def sib_copy(g, j):
        _, mine, other = groups[g]
        return remote(region(mine, j), region(other, j), sib_ss.at[g, j], sib_rs.at[g, j], sibling)

    def gather_weights(g, t):
        if t == 0:
            for k in range(1, n):
                for copy in piece_copies(g, k):
                    copy.wait_recv()
            pl.when(has_up)(lambda: up_copy(g, 0, i).start())
            pl.when(has_down)(lambda: down_copy(g, 0, i).start())
            sib_copy(g, i).start()
            return

        @pl.when(i - t >= 0)
        def _():
            up_copy(g, t - 1, i - t).wait_recv()
            if t < m - 1:
                pl.when(has_up)(lambda: up_copy(g, t, i - t).start())
            sib_copy(g, i - t).start()

        @pl.when(i + t < m)
        def _():
            down_copy(g, t - 1, i + t).wait_recv()
            if t < m - 1:
                pl.when(has_down)(lambda: down_copy(g, t, i + t).start())
            sib_copy(g, i + t).start()

    def x_copy(k):
        return remote(x_hbm, x_all.at[k], x_ss.at[k], x_rs.at[k], peers[k])

    def dy_copy(k):
        return remote(dy_hbm, dy_all.at[k], dy_ss.at[k], dy_rs.at[k], peers[k])

    def hn_copy(k):
        return remote(hn_all.at[0], hn_all.at[k], hn_ss.at[k], hn_rs.at[k], peers[k])

    def part_copy(k):
        return remote(part_s.at[k], part_r.at[k], part_ss.at[k], part_rs.at[k], peers[k])

    load_x = pltpu.make_async_copy(x_hbm, x_all.at[0], load_sem.at[0])
    load_wo = pltpu.make_async_copy(wo_hbm, wo, load_sem.at[1])
    load_dy = pltpu.make_async_copy(dy_hbm, dy_v, load_sem.at[2])
    keep_dy = pltpu.make_async_copy(dy_v, dy_all.at[0], load_sem.at[3])

    load_x.start()
    for k in range(1, n):
        for copy in piece_copies(0, k):
            copy.start()
    for k in range(1, n):
        x_copy(k).start()
    for copy in own_copies(0):
        copy.start()
    for k in range(1, n):
        for copy in piece_copies(1, k):
            copy.start()
    for copy in own_copies(1):
        copy.start()
    load_wo.start()
    load_dy.start()

    def place(k, h, kk):
        return pl.ds(
            pl.multiple_of((shard ^ kk) * own + (core if h == 0 else 1 - core) * half, half), half
        )

    gather_weights(0, 0)
    for k in range(n):
        if k == 0:
            load_x.wait()
        else:
            x_copy(k).wait_recv()
        v = x_all[k].astype(F32)
        r = lax.rsqrt(jnp.mean(v * v, -1, keepdims=True) + EPSILON)
        for h in range(2):
            for kk in range(n):
                at = place(k, h, kk)
                normed[k * rows : (k + 1) * rows, (h * n + kk) * half : (h * n + kk + 1) * half] = (
                    x_all[k, :, at].astype(F32) * r * ag[:, at]
                ).astype(BF)
    for t in range(1, m - 1):
        gather_weights(0, t)
    gather_weights(1, 0)
    gather_weights(0, m - 1)
    for copy in own_copies(0):
        copy.wait()
    for j in range(m):
        sib_copy(0, j).wait_recv()

    cols = qkv.shape[1]
    step = min(cols, 256)

    @pl.loop(0, cols // step)
    def _(b):
        at = pl.ds(pl.multiple_of(b * step, step), step)
        both = n * half
        qkv[:, at] = dot(
            normed[:, :both], qkv_mine[:, :, :, at].reshape(both, step)
        ) + dot(normed[:, both:], qkv_other[:, :, :, at].reshape(both, step))

    hop = 1
    for copy in own_copies(1):
        copy.wait()
    for copy in back_copies():
        copy.start()
    load_dy.wait()
    keep_dy.start()
    for j in range(nk):
        attend_pair(qkv, j, nq, nk, qg, kg, cos2, sin2, trow, tcol, o, qr, kr, vb, scale)
        if j == 0 and hop < m - 1:
            gather_weights(1, hop)
            hop += 1

    load_wo.wait()
    step = min(width, 512)

    @pl.loop(0, width // step)
    def _(b):
        at = pl.ds(pl.multiple_of(b * step, step), step)
        for k in range(n):
            value = dot(o[k * rows : (k + 1) * rows, :], wo[:, at])
            if k == 0:
                part_own[:, at] = value
            else:
                part_s[k, :, at] = value.astype(BF)

    for k in range(1, n):
        part_copy(k).start()
    if hop < m - 1:
        gather_weights(1, hop)
        hop += 1
    total = x_all[0].astype(F32) + part_own[...]
    for k in range(1, n):
        part_copy(k).wait_recv()
        total = total + part_r[k].astype(F32)
    hidden[...] = total
    r = lax.rsqrt(jnp.mean(total * total, -1, keepdims=True) + EPSILON)
    hn_all[0] = (total * r * mg[...]).astype(BF)
    for k in range(1, n):
        hn_copy(k).start()
    for k in range(1, n):
        dy_copy(k).start()
    while hop < m - 1:
        gather_weights(1, hop)
        hop += 1
    for k in range(n):
        if k > 0:
            hn_copy(k).wait_recv()
        for h in range(2):
            for kk in range(n):
                hn[k * rows : (k + 1) * rows, (h * n + kk) * half : (h * n + kk + 1) * half] = (
                    hn_all[k, :, place(k, h, kk)]
                )
    gather_weights(1, m - 1)

    for copy in back_copies():
        copy.wait()
    keep_dy.wait()
    for k in range(1, n):
        for g in range(2):
            for copy in piece_copies(g, k):
                copy.wait_send()
        x_copy(k).wait_send()
        part_copy(k).wait_send()
        hn_copy(k).wait_send()
        dy_copy(k).wait_send()
        dy_copy(k).wait_recv()
    for g in range(2):
        for j in range(m):
            sib_copy(g, j).wait_send()
            if g == 1:
                sib_copy(g, j).wait_recv()
        for t in range(m - 1):
            pl.when((i - t >= 0) & has_up)(lambda: up_copy(g, t, i).wait_send())
            pl.when((i + t < m) & has_down)(lambda: down_copy(g, t, i).wait_send())


def front(n, m, nq, nk, x, dy, weights, wo, gains, tables):
    rows, width = x.shape
    length = n * rows
    q = weights[0].shape[2]
    cols = [sum(w.shape[3] // n for w in ws) for ws in (weights[:3], weights[3:])]
    vmem, hbm = pl.BlockSpec(memory_space=pltpu.VMEM), pl.BlockSpec(memory_space=pl.ANY)
    dma = pltpu.SemaphoreType.DMA
    sd = jax.ShapeDtypeStruct
    outs = [
        (sd((length, width), BF), vmem),
        (sd((length, cols[0]), F32), vmem),
        (sd((length, nq * HD), BF), vmem),
        (sd((length, nk * HD), BF), vmem),
        (sd((length, nk * HD), BF), vmem),
        (sd((length, nq * HD), BF), vmem),
        (sd((rows, width), F32), vmem),
        (sd((length, width), BF), vmem),
        (sd((n, m, q, cols[0]), BF), vmem),
        (sd((n, m, q, cols[0]), BF), vmem),
        (sd((n, m, q, cols[1]), BF), hbm),
        (sd((n, m, q, cols[1]), BF), hbm),
        (sd((n, rows, width), BF), hbm),
    ]
    return pl.pallas_call(
        partial(front_kernel, n, m, nq, nk, 1.0 / math.sqrt(HD)),
        out_shape=tuple(v[0] for v in outs),
        in_specs=[hbm] * 8 + [vmem] * 8,
        out_specs=tuple(v[1] for v in outs),
        scratch_shapes=[
            pltpu.VMEM((n, rows, width), BF),
            pltpu.VMEM(wo.shape, BF),
            pltpu.VMEM((2, m, q, cols[1]), BF),
            pltpu.VMEM((rows, width), BF),
            pltpu.VMEM((n, rows, width), BF),
            pltpu.VMEM((rows, width), F32),
            pltpu.VMEM((n, rows, width), BF),
            pltpu.VMEM((n, rows, width), BF),
            dma((n,)), dma((n,)),
            dma((2, n, 3)), dma((2, n, 3)),
            dma((2, m)), dma((2, m)), dma((2, m)), dma((2, m)), dma((2, m)), dma((2, m)),
            dma((2, 2, 3)), dma((2,)), dma((4,)),
            dma((n,)), dma((n,)), dma((n,)), dma((n,)), dma((n,)), dma((n,)),
        ],
        compiler_params=pltpu.CompilerParams(
            collective_id=1, has_side_effects=True, vmem_limit_bytes=60 << 20
        ),
        name="front",
    )(x, dy, *weights, wo, *gains, *tables)


def build(n, reps):
    m = reps // 2

    def per_device(
        activations, segments, attn_gain, query_weight, key_weight, value_weight,
        query_gain, key_gain, out_weight, mlp_gain, gate_weight, up_weight, down_weight,
        cotangent,
    ):
        rows, width = activations.shape[1], activations.shape[2]
        length = segments.shape[1]
        shard = lax.axis_index("shard")
        core = lax.axis_index("rep") % 2
        own = width // n
        half = own // 2
        nq, nk = HQ // n, HK // n
        ffl = FF // n
        owner = [shard ^ k for k in range(n)]

        def cut(v, start, size, axis):
            return lax.dynamic_slice_in_dim(v, start, size, axis)

        def times(v, w):
            both = v.shape[1] // 2
            return dot(v[:, :both], w[0]) + dot(v[:, both:], w[1])

        seg_ids = segments[0]
        pos = positions(seg_ids)
        tokens = jnp.arange(length, dtype=jnp.int32)
        shuffle = lambda v: jnp.concatenate([cut(v, owner[k] * rows, rows, 0) for k in range(n)])
        index, seg_ids, pos = shuffle(tokens), shuffle(seg_ids), shuffle(pos)
        inv_freq = 1.0 / ROPE_BASE ** (jnp.arange(HD // 2, dtype=F32) * (2.0 / HD))
        angles = pos[:, None] * inv_freq[None, :]
        cosine, sine = jnp.cos(angles), jnp.sin(angles)
        cos2 = jnp.concatenate([cosine, cosine], 1)
        sin2 = jnp.concatenate([-sine, sine], 1)
        tcol = jnp.stack([index, seg_ids], 0)
        trow = jnp.stack([index, seg_ids], 1)
        qg, kg = query_gain[None], key_gain[None]

        cut_rows = lambda w: w.reshape(2, m, half // m, w.shape[1])
        (
            normed, qkv, qr, kr, vb, attn_out, hidden, normed_mlp,
            qkv_mine, qkv_other, mlp_mine, mlp_other, all_grads,
        ) = front(
            n, m, nq, nk, activations[0], cotangent[0],
            [cut_rows(w) for w in (query_weight, key_weight, value_weight, gate_weight, up_weight)],
            out_weight,
            [attn_gain[None], qg, kg, mlp_gain[None]],
            [cos2, sin2, trow, tcol],
        )
        w_mlp = [v.reshape(n * half, -1) for v in (mlp_mine, mlp_other)]
        flat_grads = all_grads.reshape(length, width)
        pre = times(normed_mlp, w_mlp)
        gate_pre, up_pre = pre[:, :ffl], pre[:, ffl:]
        sig = jax.nn.sigmoid(gate_pre)
        activated = (gate_pre * sig * up_pre).astype(BF)
        grad_act = dot_last(flat_grads, down_weight)
        grad_gate = (grad_act * up_pre * sig * (1.0 + gate_pre * (1.0 - sig))).astype(BF)
        grad_up = (grad_act * gate_pre * sig).astype(BF)
        grad_pre = jnp.concatenate([grad_gate, grad_up], 1)
        output, grad_input, gains, *summed = back(
            n, m, nq, nk, activations[0], hidden, out_weight, down_weight,
            [qkv_mine, qkv_other, mlp_mine, mlp_other], qkv, [qr, kr, vb], attn_out, normed,
            normed_mlp, activated, all_grads, grad_pre,
            [attn_gain[None], mlp_gain[None], qg, kg], [cos2, sin2, trow, tcol],
        )
        output, grad_input = output[None], grad_input[None]
        mines, others = summed[:4], summed[4:]

        pick = lambda seg, at=None, width=None: (
            (mines[seg], others[seg]) if at is None else (mines[seg], others[seg], at, width)
        )
        (
            grad_down, grad_out_weight, grad_gate_weight, grad_up_weight,
            grad_query_weight, grad_key_weight, grad_value_weight,
        ) = assemble(
            [pick(0), pick(2)],
            [
                pick(1, 0, ffl), pick(1, 1, ffl), pick(3, 0, nq * HD),
                pick(3, nq // nk, nk * HD), pick(3, nq // nk + 1, nk * HD),
            ],
            core,
            owner,
        )
        gains = gains.reshape(-1)
        grad_attn_gain, grad_mlp_gain = gains[:width], gains[width : 2 * width]
        grad_query_gain = gains[2 * width : 2 * width + HD]
        grad_key_gain = gains[2 * width + HD : 2 * width + 2 * HD]
        return (
            output,
            grad_input,
            grad_attn_gain,
            grad_query_weight,
            grad_key_weight,
            grad_value_weight,
            grad_query_gain,
            grad_key_gain,
            grad_out_weight,
            grad_mlp_gain,
            grad_gate_weight,
            grad_up_weight,
            grad_down,
        )

    return per_device


def solution(mesh):
    tok = P("rep", "shard", None)
    row = P("shard", None)
    return jax.shard_map(
        build(mesh.shape["shard"], mesh.shape["rep"]),
        mesh=mesh,
        in_specs=(
            tok, P("rep", None), P(), row, row, row, P(), P(), row, P(), row, row, row, tok,
        ),
        out_specs=(tok, tok, P(), row, row, row, P(), P(), row, P(), row, row, row),
        check_vma=False,
    )
```

profile of v0, /device:TPU:0, one launch (start us, length us, event | category | flops | bytes accessed | tf_op | source)
XLA Modules:
  0.0 564.0 jit_solution(2988301026520691525)
XLA Ops:
  0.7 0.7 stack.47.order_ref
  1.3 0.8 add_select_fusion
  2.2 0.3 reduce-window.9
  2.5 0.1 slice.51
  2.6 0.1 slice_reduce_fusion
  2.7 0.1 fusion.5
  2.8 0.1 fusion.10
  2.9 0.1 dynamic_slice.51
  3.0 0.7 fusion.6
  3.7 0.1 dynamic_slice.50
  3.8 0.1 dynamic_slice.49
  3.9 0.1 dynamic_slice.48
  3.9 0.6 pad_add_fusion.1.tcol.refs_25_
  4.6 0.9 copy.29.trow.refs_24_
  5.4 1.0 fusion.3
  6.4 1.0 pad_maximum_fusion.1
  7.4 161.1 %front.1 = (bf16[512,2048]{1,0:T(8,128)(2,1)}, f32[512,1024]{1,0:T(8,128)}, bf16[512,512]{1,0:T(8,128)(2,1)}, bf16[512,256]{1,0:T(8,128)(2,1)}, bf16[512,256]{1,...) custom-call(bf16[128,2048]{1,0:T(8,128)(2,1)} %bitcast.64, ...), custom_call_target="tpu_custom_call" | custom-call | tf_op jit(solution)/shard_map/front/pallas_call | solution.py:1002
  168.6 0.0 copy-start
  168.6 0.0 copy-start.1
  168.6 0.0 slice-start
  168.6 5.9 %fusion.1 = f32[512,3072]{1,0:T(8,128)S(1)} fusion(bf16[1024,3072]{1,0:T(8,128)(2,1)} %bitcast.62, bf16[512,2048]{1,0:T(8,128)(2,1)} %get-tuple-element.55.refs_14_), kind=kOutput, calls=%fused_computation.7 | convolution fusion | flops 3221225472 | bytes 13631488 | tf_op jit(solution)/shard_map/dot_general | solution.py:27
  174.6 0.0 copy-done
  174.6 0.0 copy-done.1
  174.6 0.0 slice-start.1
  174.6 0.0 copy-start.2
  174.6 3.5 convolution_add_fusion
  178.1 0.0 slice-done
  178.1 0.0 slice-done.1
  178.1 0.0 copy-done.2
  178.1 5.9 %multiply_convert_fusion.1 = (bf16[512,1536]{1,0:T(8,128)(2,1)S(1)}, bf16[512,1536]{1,0:T(8,128)(2,1)S(1)}, bf16[512,1536]{1,0:T(8,128)(2,1)}) fusion(f32[512,3072]{1,0:T(8,128)S(1)} %convolution_add_fusion, bf16[512,2048]{1,0:T(8,128)(2,1)S(1)} %bitcast.67, bf16[1536,2048]{1,0:T(8,128)(2,1)S(1)} %bitcast.61), kind=kOutput, calls=%fused_computation.3 | convolution fusion | flops 3233808384 | bytes 19398656 | tf_op jit(solution)/shard_map/dot_general | solution.py:31
  184.0 2.1 pad_maximum_fusion.refs_17_
  186.2 346.8 %back.1 = (bf16[128,2048]{1,0:T(8,128)(2,1)}, f32[128,2048]{1,0:T(8,128)}, f32[40,128]{1,0:T(8,128)}, bf16[4,3,64,2048]{3,2,1,0:T(8,128)(2,1)}, bf16[4,4,64,3072...) custom-call(bf16[128,2048]{1,0:T(8,128)(2,1)} %bitcast.65, ...), custom_call_target="tpu_custom_call" | custom-call | tf_op jit(solution)/shard_map/back/pallas_call | solution.py:676
  533.0 1.3 slice_bitcast_fusion.2
  534.2 1.3 slice_bitcast_fusion
  535.6 0.0 copy-start.4
  535.6 0.0 copy-start.3
  535.6 26.2 %assemble.1 = (f32[1536,2048]{1,0:T(8,128)}, f32[512,2048]{1,0:T(8,128)}, f32[512,6144]{1,0:T(8,128)}, f32[512,6144]{1,0:T(8,128)}, f32[512,2048]{1,0:T(8,128)},...) custom-call(s32[5]{0:T(128)} %stack.47.order_ref, bf16[4,3,64,2048]{3,2,1,0:T(8,128)(2,1)} %get-tuple-element.60.refs_0_, ...), custom_call_target="tpu_custom_call" | custom-call | bytes 75497472 | tf_op jit(solution)/shard_map/assemble/pallas_call | solution.py:176
  561.8 0.0 copy-done.4
  561.8 0.8 copy.33
  562.6 0.0 copy-done.3
  562.6 1.0 copy.34
  (11 shorter events, 0.1 us)
Async XLA Ops:
  168.6 6.0 %copy-start = (bf16[4,4,64,3072]{3,2,1,0:T(8,128)(2,1)S(1)}, bf16[4,4,64,3072]{3,2,1,0:T(8,128)(2,1)}, u32[]{:S(2)}) copy-start(bf16[4,4,64,3072]{3,2,1,0:T(8,128)(2,1)} %get-tuple-element.48.refs_7_) | copy-start | bytes 18874372
  168.6 6.0 %copy-start.1 = (bf16[512,2048]{1,0:T(8,128)(2,1)S(1)}, bf16[512,2048]{1,0:T(8,128)(2,1)}, u32[]{:S(2)}) copy-start(bf16[512,2048]{1,0:T(8,128)(2,1)} %get-tuple-element.55.refs_14_) | copy-start | bytes 6291460
  168.6 9.5 %slice-start = ((s8[6291456]{0:T(1024)(128)(4,1)}), s8[4194304]{0:T(1024)(128)(4,1)S(1)}, s32[]{:S(2)}) async-start(s8[6291456]{0:T(1024)(128)(4,1)} %bitcast.60), calls=%async_computation | async-start | bytes 8388608
  174.6 3.5 slice-start.1
  174.6 3.5 copy-start.2
  535.6 26.2 %copy-start.4 = (bf16[128,2048]{1,0:T(8,128)(2,1)S(1)}, bf16[128,2048]{1,0:T(8,128)(2,1)}, u32[]{:S(2)}) copy-start(bf16[128,2048]{1,0:T(8,128)(2,1)} %get-tuple-element.57) | copy-start | bytes 1572868
  535.6 27.0 %copy-start.3 = (f32[128,2048]{1,0:T(8,128)S(1)}, f32[128,2048]{1,0:T(8,128)}, u32[]{:S(2)}) copy-start(f32[128,2048]{1,0:T(8,128)} %get-tuple-element.58) | copy-start | bytes 3145732
where the time goes:
time: 572 us; the launch traced here: 564 us
  Pallas kernels  534 us (93%)
  matrix products  15.3 us (3%)
  local copies, waits for them, and re-layouts  7.21 us (1%)
  other arithmetic  6.02 us (1%)
    pallas_call x1, Pallas kernels, back(): pl.pallas_call(partial(back_kernel, n, m, nq, nk, 1.0 / math.sqrt(HD), pa...  347 us
    pallas_call x1, Pallas kernels, front(): pl.pallas_call(partial(front_kernel, n, m, nq, nk, 1.0 / math.sqrt(HD)),...  161 us
    pallas_call x1, Pallas kernels, assemble(): pl.pallas_call(partial(assemble_kernel, (len(rows), len(cols))), out_shap...  26.2 us

commit v1 on v0

--- a/solution.py
+++ b/solution.py
@@ -20,7 +20,7 @@
 BF = jnp.bfloat16
 F32 = jnp.float32
 
-HOOK_TICKS = (0, 4, 6, 7, 8, 9, 11, 12, 13, 14, 15, 16, 18)
+DHN_TICK = 1
 
 
 def dot(a, b):
@@ -69,7 +69,7 @@
             seen = (tcol[0:1, :] <= trow[rows, 0:1]) & (tcol[1:2, :] == trow[rows, 1:2])
             s = jnp.where(seen, s, MASKED)
             e = jnp.exp(s - jnp.max(s, -1, keepdims=True))
-            p = (e / jnp.sum(e, -1, keepdims=True)).astype(BF)
+            p = (e * (1.0 / jnp.sum(e, -1, keepdims=True))).astype(BF)
             o_ref[rows, cols] = dot(p, vb).astype(BF)
 
 
@@ -103,7 +103,7 @@
             seen = (tcol[0:1, :] <= trow[rows, 0:1]) & (tcol[1:2, :] == trow[rows, 1:2])
             s = jnp.where(seen, s, MASKED)
             e = jnp.exp(s - jnp.max(s, -1, keepdims=True))
-            p = e / jnp.sum(e, -1, keepdims=True)
+            p = e * (1.0 / jnp.sum(e, -1, keepdims=True))
             dp = dot_last(do, vb)
             ds = (p * (dp - jnp.sum(p * dp, -1, keepdims=True))).astype(BF)
             dqr.append(dot(ds, kr) * scale)
@@ -477,7 +477,7 @@
 
         strips(body)
 
-    def partial_rows(grads, mine, other):
+    def partial_rows(grads, mine, other, turn):
         cols = grads.shape[1]
 
         def tile_copy(b):
@@ -486,8 +486,9 @@
                 src, wtile.at[b % 2, :, :, pl.ds(0, cols)], wt_sem.at[b % 2]
             )
 
-        tile_copy(0).start()
-        for b in range(2 * n):
+        if turn == 0:
+            tile_copy(0).start()
+        for b in (2 * turn, 2 * turn + 1):
             tile_copy(b).wait()
             if b + 1 < 2 * n:
                 tile_copy(b + 1).start()
@@ -500,11 +501,13 @@
             for k in range(n):
                 part_s[k, :, at] = dot_last(grads[k * rows : (k + 1) * rows, :], w).astype(BF)
 
-    def hook_dhn():
-        loads[2].wait()
-        partial_rows(dpre, mlp_mine, mlp_other)
-        for k in range(1, n):
-            dhn_copy(k).start()
+    def hook_dhn(turn):
+        if turn == 0:
+            loads[2].wait()
+        partial_rows(dpre, mlp_mine, mlp_other, turn)
+        if turn == n - 1:
+            for k in range(1, n):
+                dhn_copy(k).start()
 
     def hook_hidden():
         loads[4].wait()
@@ -536,12 +539,14 @@
         add_gain(2 * width // HD, gq)
         add_gain(2 * width // HD + 1, gk)
 
-    def hook_normed():
-        for k in range(1, n):
-            dhn_copy(k).wait_send()
-        partial_rows(dqkv, qkv_mine, qkv_other)
-        for k in range(1, n):
-            dn_copy(k).start()
+    def hook_normed(turn):
+        if turn == 0:
+            for k in range(1, n):
+                out_copy(k).wait_send()
+        partial_rows(dqkv, qkv_mine, qkv_other, turn)
+        if turn == n - 1:
+            for k in range(1, n):
+                dn_copy(k).start()
 
     def hook_input():
         for k in range(1, n):
@@ -552,9 +557,10 @@
 
         norm_back(x_v, ag, 0, result)
 
-    def hook_down():
-        for k in range(1, n):
-            dn_copy(k).wait_send()
+    def hook_down(turn):
+        if turn == 0:
+            for k in range(1, n):
+                dhn_copy(k).wait_send()
         step = dtile.shape[2]
 
         def tile_copy(b):
@@ -562,17 +568,20 @@
                 wd_hbm.at[:, pl.ds(b * step, step)], dtile.at[b % 2], wt_sem.at[b % 2]
             )
 
-        tile_copy(0).start()
-        for b in range(width // step):
+        count = width // step
+        if turn == 0:
+            tile_copy(0).start()
+        for b in range(turn * count // 2, (turn + 1) * count // 2):
             tile_copy(b).wait()
-            if b + 1 < width // step:
+            if b + 1 < count:
                 tile_copy(b + 1).start()
             for k in range(n):
                 part_s[k, :, b * step : (b + 1) * step] = dot(
                     act[k * rows : (k + 1) * rows, :], dtile[b % 2]
                 ).astype(BF)
-        for k in range(1, n):
-            out_copy(k).start()
+        if turn == 1:
+            for k in range(1, n):
+                out_copy(k).start()
 
     def hook_output():
         for k in range(1, n):
@@ -587,11 +596,18 @@
         strips(body)
 
     at_tick = {}
-    hooks = [hook_dhn, hook_hidden, hook_do] + [partial(hook_head, j) for j in range(nk)]
-    hooks += [hook_normed, hook_input] + [partial(gains, level) for level in range(4)]
-    hooks += [hook_down, hook_output]
-    for hook, tick in zip(hooks, HOOK_TICKS[:3] + HOOK_TICKS[3 : 3 + nk] + HOOK_TICKS[-8:]):
-        at_tick.setdefault(tick, []).append(hook)
+    def plan(tick, *pieces):
+        for f, piece in enumerate(pieces):
+            at_tick.setdefault(tick + f, []).append(piece)
+
+    plan(DHN_TICK, *[partial(hook_dhn, turn) for turn in range(n)])
+    tick = DHN_TICK + n + 2
+    plan(tick, hook_hidden, partial(hook_down, 0), partial(hook_down, 1), hook_do)
+    tick += 4
+    plan(tick, *[partial(hook_head, j) for j in range(nk)])
+    plan(tick + nk, hook_output, *[partial(hook_normed, turn) for turn in range(n)])
+    tick += nk + n + 3
+    plan(tick, hook_input, *[partial(gains, level) for level in range(4)])
 
     stages = [first] + [lambda p, t=t: scatter_step(p, t) for t in range(1, m - 1)]
     stages += [total] + [lambda p, t=t: gather_step(p, t) for t in range(m)]
@@ -615,7 +631,7 @@
 
     for k in range(1, n):
         dz_copy(k).wait_send()
-        out_copy(k).wait_send()
+        dn_copy(k).wait_send()
     for level in range(3):
         for copy in gain_copies(level):
             copy.wait_send()
@@ -712,10 +728,12 @@
     n, m, nq, nk, scale,
     x_hbm, dy_hbm, wq, wk, wv, wg, wu, wo_hbm,
     ag, qg, kg, mg, cos2, sin2, trow, tcol,
-    normed, qkv, qr, kr, vb, o, hidden, hn, qkv_mine, qkv_other, mlp_mine, mlp_other, dy_all,
+    normed_hbm, qkv_hbm, qr_hbm, kr_hbm, vb_hbm, o_hbm, hidden_hbm, hn_hbm,
+    qkv_mine_hbm, qkv_other_hbm, mlp_mine, mlp_other, dy_all,
+    normed, qkv, qr, kr, vb, o, hidden, hn, qkv_mine, qkv_other,
     x_all, wo, bounce, dy_v, hn_all, part_own, part_s, part_r,
     x_ss, x_rs, w_ss, w_rs, up_ss, up_rs, down_ss, down_rs, sib_ss, sib_rs,
-    own_sem, back_sem, load_sem, part_ss, part_rs, hn_ss, hn_rs, dy_ss, dy_rs
+    own_sem, back_sem, load_sem, part_ss, part_rs, hn_ss, hn_rs, dy_ss, dy_rs, store_sem
 ):
     shard, rep = lax.axis_index("shard"), lax.axis_index("rep")
     i = rep // 2
@@ -746,13 +764,23 @@
             device_id=dev, device_id_type=MESH_ID,
         )
 
+    results = [
+        (normed, normed_hbm), (qkv_mine, qkv_mine_hbm), (qkv_other, qkv_other_hbm),
+        (qkv, qkv_hbm), (qr, qr_hbm), (kr, kr_hbm), (vb, vb_hbm), (o, o_hbm), (hidden, hidden_hbm),
+    ] + [(hn.at[pl.ds(k * rows, rows)], hn_hbm.at[pl.ds(k * rows, rows)]) for k in range(n)]
+    stores = [
+        pltpu.make_async_copy(src, dst, store_sem.at[f]) for f, (src, dst) in enumerate(results)
+    ]
+
+    ffl = wg.shape[3] // n
     groups = [
-        ([wq, wk, wv], qkv_mine, qkv_other),
-        ([wg, wu], mlp_mine, mlp_other),
+        ([wq, wk, wv], qkv_mine, qkv_other, 0, qkv.shape[1]),
+        ([wg], mlp_mine, mlp_other, 0, ffl),
+        ([wu], mlp_mine, mlp_other, ffl, ffl),
     ]
 
-    def fields(weights):
-        at = 0
+    def fields(g):
+        weights, _, _, at, _ = groups[g]
         for w in weights:
             size = w.shape[3] // n
             yield w, at, size
@@ -762,21 +790,21 @@
         return pl.ds(pl.multiple_of((shard ^ k) * size, size), size)
 
     def piece_copies(g, k):
-        weights, mine, _ = groups[g]
+        mine = groups[g][1]
         return [
             remote(
                 w.at[core, i, :, cols_of(k, size)],
                 mine.at[k, i, :, pl.ds(at, size)],
                 w_ss.at[g, k, f], w_rs.at[g, k, f], peers[k],
             )
-            for f, (w, at, size) in enumerate(fields(weights))
+            for f, (w, at, size) in enumerate(fields(g))
         ]
 
     def own_copies(g):
-        weights, mine, other = groups[g]
+        mine, other = groups[g][1:3]
         out = []
         for h, dst in enumerate((mine, other)):
-            for f, (w, at, size) in enumerate(fields(weights)):
+            for f, (w, at, size) in enumerate(fields(g)):
                 to = dst.at[0, :, :, pl.ds(at, size)] if g == 0 else bounce.at[h, :, :, pl.ds(at, size)]
                 src = w.at[core if h == 0 else 1 - core, :, :, cols_of(0, size)]
                 out.append(pltpu.make_async_copy(src, to, own_sem.at[g, h, f]))
@@ -788,20 +816,21 @@
             for h, dst in enumerate((mlp_mine, mlp_other))
         ]
 
-    def region(ref, j):
-        return ref.at[pl.ds(1, n - 1), j]
+    def region(g, ref, j):
+        at, size = groups[g][3:]
+        return ref.at[pl.ds(1, n - 1), j, :, pl.ds(at, size)]
 
     def up_copy(g, t, j):
-        r = region(groups[g][1], j)
+        r = region(g, groups[g][1], j)
         return remote(r, r, up_ss.at[g, t], up_rs.at[g, t], above)
 
     def down_copy(g, t, j):
-        r = region(groups[g][1], j)
+        r = region(g, groups[g][1], j)
         return remote(r, r, down_ss.at[g, t], down_rs.at[g, t], below)
 
     def sib_copy(g, j):
-        _, mine, other = groups[g]
-        return remote(region(mine, j), region(other, j), sib_ss.at[g, j], sib_rs.at[g, j], sibling)
+        mine, other = groups[g][1:3]
+        return remote(region(g, mine, j), region(g, other, j), sib_ss.at[g, j], sib_rs.at[g, j], sibling)
 
     def gather_weights(g, t):
         if t == 0:
@@ -844,26 +873,38 @@
     load_dy = pltpu.make_async_copy(dy_hbm, dy_v, load_sem.at[2])
     keep_dy = pltpu.make_async_copy(dy_v, dy_all.at[0], load_sem.at[3])
 
+    def start_pieces(g):
+        for k in range(1, n):
+            for copy in piece_copies(g, k):
+                copy.start()
+
     load_x.start()
-    for k in range(1, n):
-        for copy in piece_copies(0, k):
-            copy.start()
+    start_pieces(0)
+    start_pieces(1)
     for k in range(1, n):
         x_copy(k).start()
     for copy in own_copies(0):
         copy.start()
+    start_pieces(2)
     for k in range(1, n):
-        for copy in piece_copies(1, k):
+        dy_copy(k).start()
+    load_wo.start()
+    for g in (1, 2):
+        for copy in own_copies(g):
             copy.start()
-    for copy in own_copies(1):
-        copy.start()
-    load_wo.start()
     load_dy.start()
 
     def place(k, h, kk):
         return pl.ds(
             pl.multiple_of((shard ^ kk) * own + (core if h == 0 else 1 - core) * half, half), half
         )
+
+    hops = [(1, t) for t in range(1, m)] + [(2, t) for t in range(m)]
+    hops.sort(key=lambda v: 2 * v[1] + v[0])
+
+    def next_hops(count):
+        for _ in range(min(count, len(hops))):
+            gather_weights(*hops.pop(0))
 
     gather_weights(0, 0)
     for k in range(n):
@@ -879,14 +920,20 @@
                 normed[k * rows : (k + 1) * rows, (h * n + kk) * half : (h * n + kk + 1) * half] = (
                     x_all[k, :, at].astype(F32) * r * ag[:, at]
                 ).astype(BF)
-    for t in range(1, m - 1):
+        if k + 1 < m - 1:
+            gather_weights(0, k + 1)
+        if k == min(n, m - 1) - 1:
+            gather_weights(1, 0)
+    for t in range(n + 1, m - 1):
         gather_weights(0, t)
-    gather_weights(1, 0)
+    stores[0].start()
     gather_weights(0, m - 1)
     for copy in own_copies(0):
         copy.wait()
     for j in range(m):
         sib_copy(0, j).wait_recv()
+    stores[1].start()
+    stores[2].start()
 
     cols = qkv.shape[1]
     step = min(cols, 256)
@@ -899,18 +946,20 @@
             normed[:, :both], qkv_mine[:, :, :, at].reshape(both, step)
         ) + dot(normed[:, both:], qkv_other[:, :, :, at].reshape(both, step))
 
-    hop = 1
-    for copy in own_copies(1):
-        copy.wait()
+    stores[3].start()
+    for g in (1, 2):
+        for copy in own_copies(g):
+            copy.wait()
     for copy in back_copies():
         copy.start()
     load_dy.wait()
     keep_dy.start()
     for j in range(nk):
         attend_pair(qkv, j, nq, nk, qg, kg, cos2, sin2, trow, tcol, o, qr, kr, vb, scale)
-        if j == 0 and hop < m - 1:
-            gather_weights(1, hop)
-            hop += 1
+        if j == 0:
+            next_hops(2)
+    for f in range(4, 8):
+        stores[f].start()
 
     load_wo.wait()
     step = min(width, 512)
@@ -927,23 +976,18 @@
 
     for k in range(1, n):
         part_copy(k).start()
-    if hop < m - 1:
-        gather_weights(1, hop)
-        hop += 1
+    next_hops(2)
     total = x_all[0].astype(F32) + part_own[...]
     for k in range(1, n):
         part_copy(k).wait_recv()
         total = total + part_r[k].astype(F32)
     hidden[...] = total
+    stores[8].start()
     r = lax.rsqrt(jnp.mean(total * total, -1, keepdims=True) + EPSILON)
     hn_all[0] = (total * r * mg[...]).astype(BF)
     for k in range(1, n):
         hn_copy(k).start()
-    for k in range(1, n):
-        dy_copy(k).start()
-    while hop < m - 1:
-        gather_weights(1, hop)
-        hop += 1
+    next_hops(len(hops) - 1)
     for k in range(n):
         if k > 0:
             hn_copy(k).wait_recv()
@@ -952,13 +996,14 @@
                 hn[k * rows : (k + 1) * rows, (h * n + kk) * half : (h * n + kk + 1) * half] = (
                     hn_all[k, :, place(k, h, kk)]
                 )
-    gather_weights(1, m - 1)
-
-    for copy in back_copies():
+        stores[9 + k].start()
+    next_hops(len(hops))
+
+    for copy in back_copies() + stores:
         copy.wait()
     keep_dy.wait()
     for k in range(1, n):
-        for g in range(2):
+        for g in range(3):
             for copy in piece_copies(g, k):
                 copy.wait_send()
         x_copy(k).wait_send()
@@ -966,10 +1011,10 @@
         hn_copy(k).wait_send()
         dy_copy(k).wait_send()
         dy_copy(k).wait_recv()
-    for g in range(2):
+    for g in range(3):
         for j in range(m):
             sib_copy(g, j).wait_send()
-            if g == 1:
+            if g > 0:
                 sib_copy(g, j).wait_recv()
         for t in range(m - 1):
             pl.when((i - t >= 0) & has_up)(lambda: up_copy(g, t, i).wait_send())
@@ -985,26 +1030,27 @@
     dma = pltpu.SemaphoreType.DMA
     sd = jax.ShapeDtypeStruct
     outs = [
-        (sd((length, width), BF), vmem),
-        (sd((length, cols[0]), F32), vmem),
-        (sd((length, nq * HD), BF), vmem),
-        (sd((length, nk * HD), BF), vmem),
-        (sd((length, nk * HD), BF), vmem),
-        (sd((length, nq * HD), BF), vmem),
-        (sd((rows, width), F32), vmem),
-        (sd((length, width), BF), vmem),
-        (sd((n, m, q, cols[0]), BF), vmem),
-        (sd((n, m, q, cols[0]), BF), vmem),
-        (sd((n, m, q, cols[1]), BF), hbm),
-        (sd((n, m, q, cols[1]), BF), hbm),
-        (sd((n, rows, width), BF), hbm),
+        sd((length, width), BF),
+        sd((length, cols[0]), F32),
+        sd((length, nq * HD), BF),
+        sd((length, nk * HD), BF),
+        sd((length, nk * HD), BF),
+        sd((length, nq * HD), BF),
+        sd((rows, width), F32),
+        sd((length, width), BF),
+        sd((n, m, q, cols[0]), BF),
+        sd((n, m, q, cols[0]), BF),
+        sd((n, m, q, cols[1]), BF),
+        sd((n, m, q, cols[1]), BF),
+        sd((n, rows, width), BF),
     ]
     return pl.pallas_call(
         partial(front_kernel, n, m, nq, nk, 1.0 / math.sqrt(HD)),
-        out_shape=tuple(v[0] for v in outs),
+        out_shape=tuple(outs),
         in_specs=[hbm] * 8 + [vmem] * 8,
-        out_specs=tuple(v[1] for v in outs),
-        scratch_shapes=[
+        out_specs=tuple([hbm] * len(outs)),
+        scratch_shapes=[pltpu.VMEM(v.shape, v.dtype) for v in outs[:10]]
+        + [
             pltpu.VMEM((n, rows, width), BF),
             pltpu.VMEM(wo.shape, BF),
             pltpu.VMEM((2, m, q, cols[1]), BF),
@@ -1014,10 +1060,10 @@
             pltpu.VMEM((n, rows, width), BF),
             pltpu.VMEM((n, rows, width), BF),
             dma((n,)), dma((n,)),
-            dma((2, n, 3)), dma((2, n, 3)),
-            dma((2, m)), dma((2, m)), dma((2, m)), dma((2, m)), dma((2, m)), dma((2, m)),
-            dma((2, 2, 3)), dma((2,)), dma((4,)),
-            dma((n,)), dma((n,)), dma((n,)), dma((n,)), dma((n,)), dma((n,)),
+            dma((3, n, 3)), dma((3, n, 3)),
+            dma((3, m)), dma((3, m)), dma((3, m)), dma((3, m)), dma((3, m)), dma((3, m)),
+            dma((3, 2, 3)), dma((2,)), dma((4,)),
+            dma((n,)), dma((n,)), dma((n,)), dma((n,)), dma((n,)), dma((n,)), dma((9 + n,)),
         ],
         compiler_params=pltpu.CompilerParams(
             collective_id=1, has_side_effects=True, vmem_limit_bytes=60 << 20

time: 572 us -> 518 us (0.906)
  Pallas kernels: 534 us -> 480 us
    pallas_call x1, Pallas kernels: 161 us -> 126 us  [front(): pl.pallas_call(partial(front_kernel, n, m, nq, nk, 1.0 / math.sqrt(HD)),...]
    pallas_call x1, Pallas kernels: 347 us -> 327 us  [back(): pl.pallas_call(partial(back_kernel, n, m, nq, nk, 1.0 / math.sqrt(HD), pa...]
where the time goes in v1:
time: 518 us; the launch traced here: 509 us
  Pallas kernels  480 us (93%)
  matrix products  15.1 us (3%)
  local copies, waits for them, and re-layouts  7.21 us (1%)
  other arithmetic  6.02 us (1%)
    pallas_call x1, Pallas kernels, back(): pl.pallas_call(partial(back_kernel, n, m, nq, nk, 1.0 / math.sqrt(HD), pa...  327 us
    pallas_call x1, Pallas kernels, front(): pl.pallas_call(partial(front_kernel, n, m, nq, nk, 1.0 / math.sqrt(HD)),...  126 us
    pallas_call x1, Pallas kernels, assemble(): pl.pallas_call(partial(assemble_kernel, (len(rows), len(cols))), out_shap...  26.2 us

profile of v1, /device:TPU:0, one launch (start us, length us, event | category | flops | bytes accessed | tf_op | source)
XLA Modules:
  0.0 509.4 jit_solution(8726279494234337868)
XLA Ops:
  0.7 0.7 stack.47.order_ref
  1.3 0.8 add_select_fusion
  2.2 0.3 reduce-window.9
  2.5 0.1 slice.51
  2.6 0.1 slice_reduce_fusion
  2.7 0.1 fusion.5
  2.8 0.1 fusion.10
  2.9 0.1 dynamic_slice.51
  3.0 0.7 fusion.6
  3.7 0.1 dynamic_slice.50
  3.8 0.1 dynamic_slice.49
  3.9 0.1 dynamic_slice.48
  3.9 0.6 pad_add_fusion.1.tcol.refs_25_
  4.6 0.9 copy.29.trow.refs_24_
  5.4 1.0 fusion.3
  6.4 1.0 pad_maximum_fusion.1
  7.4 126.4 %front.1 = (bf16[512,2048]{1,0:T(8,128)(2,1)}, f32[512,1024]{1,0:T(8,128)}, bf16[512,512]{1,0:T(8,128)(2,1)}, bf16[512,256]{1,0:T(8,128)(2,1)}, bf16[512,256]{1,...) custom-call(bf16[128,2048]{1,0:T(8,128)(2,1)} %bitcast.64, ...), custom_call_target="tpu_custom_call" | custom-call | tf_op jit(solution)/shard_map/front/pallas_call | solution.py:1047
  133.8 0.0 copy-start
  133.8 0.0 copy-start.1
  133.9 0.0 slice-start
  133.9 5.9 %fusion.1 = f32[512,3072]{1,0:T(8,128)S(1)} fusion(bf16[1024,3072]{1,0:T(8,128)(2,1)} %bitcast.62, bf16[512,2048]{1,0:T(8,128)(2,1)} %get-tuple-element.55.refs_14_), kind=kOutput, calls=%fused_computation.7 | convolution fusion | flops 3221225472 | bytes 13631488 | tf_op jit(solution)/shard_map/dot_general | solution.py:27
  139.8 0.0 copy-done
  139.8 0.0 copy-done.1
  139.8 0.0 slice-start.1
  139.9 0.0 copy-start.2
  139.9 3.5 convolution_add_fusion
  143.4 0.0 slice-done
  143.4 0.0 slice-done.1
  143.4 0.0 copy-done.2
  143.4 5.7 %multiply_convert_fusion.1 = (bf16[512,1536]{1,0:T(8,128)(2,1)S(1)}, bf16[512,1536]{1,0:T(8,128)(2,1)S(1)}, bf16[512,1536]{1,0:T(8,128)(2,1)}) fusion(f32[512,3072]{1,0:T(8,128)S(1)} %convolution_add_fusion, bf16[512,2048]{1,0:T(8,128)(2,1)S(1)} %bitcast.67, bf16[1536,2048]{1,0:T(8,128)(2,1)S(1)} %bitcast.61), kind=kOutput, calls=%fused_computation.3 | convolution fusion | flops 3233808384 | bytes 19398656 | tf_op jit(solution)/shard_map/dot_general | solution.py:31
  149.1 2.1 pad_maximum_fusion.refs_17_
  151.2 327.2 %back.1 = (bf16[128,2048]{1,0:T(8,128)(2,1)}, f32[128,2048]{1,0:T(8,128)}, f32[40,128]{1,0:T(8,128)}, bf16[4,3,64,2048]{3,2,1,0:T(8,128)(2,1)}, bf16[4,4,64,3072...) custom-call(bf16[128,2048]{1,0:T(8,128)(2,1)} %bitcast.65, ...), custom_call_target="tpu_custom_call" | custom-call | tf_op jit(solution)/shard_map/back/pallas_call | solution.py:692
  478.4 1.3 slice_bitcast_fusion.2
  479.7 1.3 slice_bitcast_fusion
  481.0 0.0 copy-start.4
  481.0 0.0 copy-start.3
  481.0 26.2 %assemble.1 = (f32[1536,2048]{1,0:T(8,128)}, f32[512,2048]{1,0:T(8,128)}, f32[512,6144]{1,0:T(8,128)}, f32[512,6144]{1,0:T(8,128)}, f32[512,2048]{1,0:T(8,128)},...) custom-call(s32[5]{0:T(128)} %stack.47.order_ref, bf16[4,3,64,2048]{3,2,1,0:T(8,128)(2,1)} %get-tuple-element.60.refs_0_, ...), custom_call_target="tpu_custom_call" | custom-call | bytes 75497472 | tf_op jit(solution)/shard_map/assemble/pallas_call | solution.py:176
  507.2 0.0 copy-done.4
  507.2 0.8 copy.33
  508.0 0.0 copy-done.3
  508.0 1.0 copy.34
  (11 shorter events, 0.1 us)
Async XLA Ops:
  133.8 6.0 %copy-start = (bf16[4,4,64,3072]{3,2,1,0:T(8,128)(2,1)S(1)}, bf16[4,4,64,3072]{3,2,1,0:T(8,128)(2,1)}, u32[]{:S(2)}) copy-start(bf16[4,4,64,3072]{3,2,1,0:T(8,128)(2,1)} %get-tuple-element.48.refs_7_) | copy-start | bytes 18874372
  133.8 6.0 %copy-start.1 = (bf16[512,2048]{1,0:T(8,128)(2,1)S(1)}, bf16[512,2048]{1,0:T(8,128)(2,1)}, u32[]{:S(2)}) copy-start(bf16[512,2048]{1,0:T(8,128)(2,1)} %get-tuple-element.55.refs_14_) | copy-start | bytes 6291460
  133.9 9.5 %slice-start = ((s8[6291456]{0:T(1024)(128)(4,1)}), s8[4194304]{0:T(1024)(128)(4,1)S(1)}, s32[]{:S(2)}) async-start(s8[6291456]{0:T(1024)(128)(4,1)} %bitcast.60), calls=%async_computation | async-start | bytes 8388608
  139.8 3.5 slice-start.1
  139.9 3.5 copy-start.2
  481.0 26.2 %copy-start.4 = (bf16[128,2048]{1,0:T(8,128)(2,1)S(1)}, bf16[128,2048]{1,0:T(8,128)(2,1)}, u32[]{:S(2)}) copy-start(bf16[128,2048]{1,0:T(8,128)(2,1)} %get-tuple-element.57) | copy-start | bytes 1572868
  481.0 27.0 %copy-start.3 = (f32[128,2048]{1,0:T(8,128)S(1)}, f32[128,2048]{1,0:T(8,128)}, u32[]{:S(2)}) copy-start(f32[128,2048]{1,0:T(8,128)} %get-tuple-element.58) | copy-start | bytes 3145732

commit v2 on v1

--- a/solution.py
+++ b/solution.py
@@ -20,7 +20,7 @@
 BF = jnp.bfloat16
 F32 = jnp.float32
 
-DHN_TICK = 1
+DHN_TICK = 2
 
 
 def dot(a, b):
@@ -52,7 +52,7 @@
 
 def attend_pair(qkv, j, nq, nk, qg, kg, cos2, sin2, trow, tcol, o_ref, qr_ref, kr_ref, vb_ref, scale):
     length = qkv.shape[0]
-    block = min(length, 512)
+    block = min(length, 256)
     own = slice(j * HD, (j + 1) * HD)
     at = (nq + j) * HD
     kr = head_rope(qkv[:, at : at + HD], kg[...], cos2[...], sin2[...]).astype(BF)
@@ -60,17 +60,22 @@
     vb = qkv[:, at : at + HD].astype(BF)
     kr_ref[:, own] = kr
     vb_ref[:, own] = vb
-    for g in range(GROUPS):
-        cols = slice((j * GROUPS + g) * HD, (j * GROUPS + g + 1) * HD)
+
+    @pl.loop(0, GROUPS)
+    def _(g):
+        cols = pl.ds(pl.multiple_of((j * GROUPS + g) * HD, HD), HD)
         qr_ref[:, cols] = head_rope(qkv[:, cols], qg[...], cos2[...], sin2[...]).astype(BF)
-        for b in range(length // block):
-            rows = slice(b * block, (b + 1) * block)
-            s = dot_last(qr_ref[rows, cols], kr) * scale
-            seen = (tcol[0:1, :] <= trow[rows, 0:1]) & (tcol[1:2, :] == trow[rows, 1:2])
+
+        @pl.loop(0, length // block)
+        def _(b):
+            rows = pl.ds(pl.multiple_of(b * block, block), block)
+            s = dot_last(qr_ref[rows, cols], kr_ref[:, own]) * scale
+            at = trow[rows, :]
+            seen = (tcol[0:1, :] <= at[:, 0:1]) & (tcol[1:2, :] == at[:, 1:2])
             s = jnp.where(seen, s, MASKED)
             e = jnp.exp(s - jnp.max(s, -1, keepdims=True))
             p = (e * (1.0 / jnp.sum(e, -1, keepdims=True))).astype(BF)
-            o_ref[rows, cols] = dot(p, vb).astype(BF)
+            o_ref[rows, cols] = dot(p, vb_ref[:, own]).astype(BF)
 
 
 def head_back(grad_rot, raw, gain, cos2, sin2):
@@ -83,42 +88,48 @@
 
 
 def attend_back_pair(
-    j, nq, nk, qkv, qr_ref, kr_ref, vb_ref, do_ref, dqkv, qg, kg, cos_ref, sin_ref, trow, tcol, scale
+    j, nq, nk, qkv, qr_ref, kr_ref, vb_ref, do_ref, dqkv, qg, kg, cos_ref, sin_ref, trow, tcol, scale,
+    sums, add_gain
 ):
-    cos2, sin2 = cos_ref[...], sin_ref[...]
     own = slice(j * HD, (j + 1) * HD)
     length = qkv.shape[0]
     block = min(length, 256)
-    kr, vb = kr_ref[:, own], vb_ref[:, own]
-    dkr = jnp.zeros((length, HD), F32)
-    dv = jnp.zeros((length, HD), F32)
-    gq = jnp.zeros((1, HD), F32)
-    for g in range(GROUPS):
-        cols = slice((j * GROUPS + g) * HD, (j * GROUPS + g + 1) * HD)
-        dqr = []
-        for b in range(length // block):
-            rows = slice(b * block, (b + 1) * block)
+    sums[1] = jnp.zeros((length, HD), F32)
+    sums[2] = jnp.zeros((length, HD), F32)
+
+    @pl.loop(0, GROUPS)
+    def _(g):
+        cols = pl.ds(pl.multiple_of((j * GROUPS + g) * HD, HD), HD)
+
+        @pl.loop(0, length // block)
+        def _(b):
+            rows = pl.ds(pl.multiple_of(b * block, block), block)
+            kr = kr_ref[:, own]
             qr, do = qr_ref[rows, cols], do_ref[rows, cols]
             s = dot_last(qr, kr) * scale
-            seen = (tcol[0:1, :] <= trow[rows, 0:1]) & (tcol[1:2, :] == trow[rows, 1:2])
+            at = trow[rows, :]
+            seen = (tcol[0:1, :] <= at[:, 0:1]) & (tcol[1:2, :] == at[:, 1:2])
             s = jnp.where(seen, s, MASKED)
             e = jnp.exp(s - jnp.max(s, -1, keepdims=True))
             p = e * (1.0 / jnp.sum(e, -1, keepdims=True))
-            dp = dot_last(do, vb)
+            dp = dot_last(do, vb_ref[:, own])
             ds = (p * (dp - jnp.sum(p * dp, -1, keepdims=True))).astype(BF)
-            dqr.append(dot(ds, kr) * scale)
-            dkr += dot_first(ds, qr)
-            dv += dot_first(p.astype(BF), do)
-        dqr = dqr[0] if len(dqr) == 1 else jnp.concatenate(dqr, 0)
-        dq, part = head_back(dqr, qkv[:, cols], qg[...], cos2, sin2)
+            sums[0, rows, :] = dot(ds, kr) * scale
+            sums[1] += dot_first(ds, qr)
+            sums[2] += dot_first(p.astype(BF), do)
+
+        dq, part = head_back(sums[0], qkv[:, cols], qg[...], cos_ref[...], sin_ref[...])
         dqkv[:, cols] = dq.astype(BF)
-        gq += part
+        add_gain(0, part)
+
     at = (nq + j) * HD
-    dk, gk = head_back(dkr * scale, qkv[:, at : at + HD], kg[...], cos2, sin2)
+    dk, part = head_back(
+        sums[1] * scale, qkv[:, at : at + HD], kg[...], cos_ref[...], sin_ref[...]
+    )
     dqkv[:, at : at + HD] = dk.astype(BF)
+    add_gain(1, part)
     at = (nq + nk + j) * HD
-    dqkv[:, at : at + HD] = dv.astype(BF)
-    return gq, gk
+    dqkv[:, at : at + HD] = sums[2].astype(BF)
 
 
 def assemble_kernel(counts, order_ref, *refs):
@@ -199,7 +210,7 @@
     mines, others, away_v, fins, refs = refs[29:33], refs[33:37], refs[37:41], refs[41:45], refs[45:]
     (ups, downs, send_v,
      x_v, hidden, wo, qkv, qr, kr, vb, o, normed, hn, act, dy_all, dpre,
-     part_s, part_r, out_r, dz_all, do, dqkv, wtile, dtile, gain_ref,
+     part_s, part_r, out_r, dz_all, do, dqkv, wtile, dtile, gain_ref, sums,
      pair_s, pair_r, up_s, up_r, down_s, down_r,
      peer_s, peer_r, gup_s, gup_r, gdown_s, gdown_r, sib_s, sib_r, own_sem, gain_pair, gain_group,
      gain_line, gain_s, gain_r, in_sem, wt_sem, dhn_s, dhn_r, dz_s, dz_r, dn_s, dn_r, out_ss,
@@ -279,8 +290,17 @@
     def down_copy(p, t, src):
         return remote(src, slot(downs, p, t), down_s.at[p, t], down_r.at[p, t], below)
 
+    def by_strips(size, body):
+        step = 16
+        pl.loop(0, size // step)(
+            lambda b: body(pl.ds(pl.multiple_of(b * step, step), step))
+        )
+
     def add_into(ref, other):
-        ref[...] = (ref[...].astype(F32) + other[...].astype(F32)).astype(BF)
+        def body(r):
+            ref[r, :] = (ref[r, :].astype(F32) + other[r, :].astype(F32)).astype(BF)
+
+        by_strips(ref.shape[0], body)
 
     def scatter_step(p, t):
         if t > 0:
@@ -312,11 +332,16 @@
         pl.when(has_up)(lambda: down_copy(p, m - 2, slot(downs, p, m - 2)).wait_recv())
         where = fin(p) if parts[p][2] == 0 else chunk(p, i)
 
+        mine = chunk(p, i)
+
         def put(*extra):
-            value = chunk(p, i)[...].astype(F32)
-            for e in extra:
-                value = value + e[...].astype(F32)
-            where[...] = value.astype(BF)
+            def body(r):
+                value = mine[r, :].astype(F32)
+                for e in extra:
+                    value = value + e[r, :].astype(F32)
+                where[r, :] = value.astype(BF)
+
+            by_strips(mine.shape[0], body)
 
         u, d = slot(ups, p, m - 2), slot(downs, p, m - 2)
         pl.when(has_up & has_down)(lambda: put(u, d))
@@ -331,8 +356,10 @@
     def gdown_copy(p, t, j, src):
         return remote(src, out(mines, p, j), gdown_s.at[p, t], gdown_r.at[p, t], below)
 
-    def sib_copy(p, j, src):
-        return remote(src, out(others, p, j), sib_s.at[p, j], sib_r.at[p, j], sibling)
+    def sib_copy(p):
+        seg, at = parts[p][:2]
+        src = mines[seg].at[:, at, :, cols_of(p)]
+        return remote(src, others[seg].at[:, at, :, cols_of(p)], sib_s.at[p], sib_r.at[p], sibling)
 
     def own_copy(p):
         return pltpu.make_async_copy(fin(p), out(mines, p, i), own_sem.at[p])
@@ -348,7 +375,6 @@
                 peer_copy(p).wait_recv()
             pl.when(has_up)(lambda: gup_copy(p, 0, i, fin(p)).start())
             pl.when(has_down)(lambda: gdown_copy(p, 0, i, fin(p)).start())
-            sib_copy(p, i, fin(p)).start()
             own_copy(p).start()
             return
 
@@ -358,7 +384,6 @@
             gup_copy(p, t - 1, i - t, here).wait_recv()
             if t < m - 1:
                 pl.when(has_up)(lambda: gup_copy(p, t, i - t, here).start())
-            sib_copy(p, i - t, here).start()
 
         @pl.when(i + t < m)
         def _():
@@ -366,7 +391,10 @@
             gdown_copy(p, t - 1, i + t, here).wait_recv()
             if t < m - 1:
                 pl.when(has_down)(lambda: gdown_copy(p, t, i + t, here).start())
-            sib_copy(p, i + t, here).start()
+
+        if t == m - 1:
+            own_copy(p).wait()
+            sib_copy(p).start()
 
     def gain_copies(level):
         if level == 0:
@@ -405,9 +433,14 @@
             for copy in gain_copies(level):
                 copy.start()
 
-    def tiles(cols, first=0):
+    def over_tiles(p, body):
+        start, cols = parts[p][3:]
         step = max(v for v in range(HD, 513, HD) if cols % v == 0)
-        return [(c, pl.ds(first + c, step), pl.ds(c, step)) for c in range(0, cols, step)]
+
+        @pl.loop(0, cols // step)
+        def _(b):
+            to = pl.multiple_of(b * step, HD)
+            body(pl.ds(pl.multiple_of(start + b * step, HD), step), pl.ds(to, step))
 
     def product(p, h, at):
         seg, place, k = parts[p][:3]
@@ -425,17 +458,23 @@
     def send(p):
         if p >= 3:
             pair_copy(p - 3).wait_send()
-        for _, at, to in tiles(parts[p][4], parts[p][3]):
+
+        def body(at, to):
             send_v[p % 3, :, :, to] = product(p, 1, at).astype(BF)
+
+        over_tiles(p, body)
         pair_copy(p).start()
 
     def first(p):
         seg, place = parts[p][:2]
         pair_copy(p).wait_recv()
-        for _, at, _ in tiles(parts[p][4], parts[p][3]):
+
+        def body(at, to):
             away_v[seg][place, :, :, at] = (
                 product(p, 0, at) + away_v[seg][place, :, :, at].astype(F32)
             ).astype(BF)
+
+        over_tiles(p, body)
         scatter_step(p, 0)
 
     def dhn_copy(k):
@@ -488,18 +527,23 @@
 
         if turn == 0:
             tile_copy(0).start()
-        for b in (2 * turn, 2 * turn + 1):
-            tile_copy(b).wait()
-            if b + 1 < 2 * n:
-                tile_copy(b + 1).start()
-            h, kk = b // n, b % n
-            at = pl.ds(
-                pl.multiple_of((shard ^ kk) * own + (core if h == 0 else 1 - core) * half, half),
-                half,
-            )
-            w = wtile[b % 2, :, :, :cols].reshape(half, cols)
-            for k in range(n):
-                part_s[k, :, at] = dot_last(grads[k * rows : (k + 1) * rows, :], w).astype(BF)
+            tile_copy(1).start()
+        tile_copy(2 * turn).wait()
+        tile_copy(2 * turn + 1).wait()
+        h, first_k = 2 * turn // n, 2 * turn % n
+
+        @pl.loop(0, 2 * n)
+        def _(f):
+            b, k = f // n, lax.rem(f, n)
+            at = (shard ^ (first_k + b)) * own + (core if h == 0 else 1 - core) * half
+            at = pl.ds(pl.multiple_of(at, half), half)
+            tokens = pl.ds(pl.multiple_of(k * rows, rows), rows)
+            w = wtile[b, :, :, :cols].reshape(half, cols)
+            part_s[k, :, at] = dot_last(grads[tokens, :], w).astype(BF)
+
+        if turn < n - 1:
+            tile_copy(2 * turn + 2).start()
+            tile_copy(2 * turn + 3).start()
 
     def hook_dhn(turn):
         if turn == 0:
@@ -527,17 +571,19 @@
     def hook_do():
         for copy in loads[5:]:
             copy.wait()
-        for k in range(n):
-            if k > 0:
-                dz_copy(k).wait_recv()
-            do[k * rows : (k + 1) * rows, :] = dot_last(dz_all[k], wo[...]).astype(BF)
+        for k in range(1, n):
+            dz_copy(k).wait_recv()
+
+        @pl.loop(0, n)
+        def _(k):
+            tokens = pl.ds(pl.multiple_of(k * rows, rows), rows)
+            do[tokens, :] = dot_last(dz_all[k], wo[...]).astype(BF)
 
     def hook_head(j):
-        gq, gk = attend_back_pair(
-            j, nq, nk, qkv, qr, kr, vb, do, dqkv, qg, kg, cos2, sin2, trow, tcol, scale
-        )
-        add_gain(2 * width // HD, gq)
-        add_gain(2 * width // HD + 1, gk)
+        attend_back_pair(
+            j, nq, nk, qkv, qr, kr, vb, do, dqkv, qg, kg, cos2, sin2, trow, tcol, scale, sums,
+            lambda f, value: add_gain(2 * width // HD + f, value),
+        )
 
     def hook_normed(turn):
         if turn == 0:
@@ -575,10 +621,14 @@
             tile_copy(b).wait()
             if b + 1 < count:
                 tile_copy(b + 1).start()
-            for k in range(n):
+
+            @pl.loop(0, n)
+            def _(k):
+                tokens = pl.ds(pl.multiple_of(k * rows, rows), rows)
                 part_s[k, :, b * step : (b + 1) * step] = dot(
-                    act[k * rows : (k + 1) * rows, :], dtile[b % 2]
+                    act[tokens, :], dtile[b % 2]
                 ).astype(BF)
+
         if turn == 1:
             for k in range(1, n):
                 out_copy(k).start()
@@ -640,14 +690,11 @@
             pair_copy(p).wait_send()
         if parts[p][2] != 0:
             peer_copy(p).wait_send()
-        own_copy(p).wait()
         for t in range(m - 1):
             pl.when((i - t >= 0) & has_up)(lambda: gup_copy(p, t, i, fin(p)).wait_send())
             pl.when((i + t < m) & has_down)(lambda: gdown_copy(p, t, i, fin(p)).wait_send())
-        for j in range(m):
-            copy = sib_copy(p, j, fin(p))
-            copy.wait_send()
-            copy.wait_recv()
+        sib_copy(p).wait_send()
+        sib_copy(p).wait_recv()
 
 
 def back(n, m, nq, nk, x, hidden, wo, wd, weights, qkv, heads, o, normed, hn, act, dy_all, dpre,
@@ -676,7 +723,7 @@
     for a in range(1, segments[0][0]):
         parts += cut(0, a, 0, [width // 2] * 2)
     for k in range(n):
-        parts += cut(1, k, k, [wide // 2] * 2)
+        parts += cut(1, k, k, [wide // 3] * 3)
     for a in range(segments[2][0]):
         parts += cut(2, a, 0, [width // 2] * 2)
     for k in range(n):
@@ -706,12 +753,12 @@
             pltpu.VMEM((n - 1, rows, width), BF), pltpu.VMEM((n, rows, width), BF),
             pltpu.VMEM((length, nq * HD), BF), pltpu.VMEM((length, cols), BF),
             pltpu.VMEM((2, m, q, wide), BF), pltpu.VMEM((2, wd.shape[0], 256), BF),
-            pltpu.VMEM(gain_shape, F32),
+            pltpu.VMEM(gain_shape, F32), pltpu.VMEM((3, length, HD), F32),
             dma((total,)), dma((total,)),
             dma((total, m - 1)), dma((total, m - 1)), dma((total, m - 1)), dma((total, m - 1)),
             dma((total,)), dma((total,)),
             dma((total, m - 1)), dma((total, m - 1)), dma((total, m - 1)), dma((total, m - 1)),
-            dma((total, m)), dma((total, m)), dma((total,)),
+            dma((total,)), dma((total,)), dma((total,)),
             pltpu.VMEM(gain_shape, F32), pltpu.VMEM((n,) + gain_shape, F32),
             pltpu.VMEM((m,) + gain_shape, F32), dma((n + m,)), dma((n + m,)),
             dma((13,)), dma((2,)),

time: 518 us -> 512 us (0.988)
  no operation moved by 1% of the time
where the time goes in v2:
time: 512 us; the launch traced here: 506 us
  Pallas kernels  476 us (93%)
  matrix products  15.1 us (3%)
  local copies, waits for them, and re-layouts  7.21 us (1%)
  other arithmetic  6.02 us (1%)
    pallas_call x1, Pallas kernels, back(): pl.pallas_call(partial(back_kernel, n, m, nq, nk, 1.0 / math.sqrt(HD), pa...  324 us
    pallas_call x1, Pallas kernels, front(): pl.pallas_call(partial(front_kernel, n, m, nq, nk, 1.0 / math.sqrt(HD)),...  126 us
    pallas_call x1, Pallas kernels, assemble(): pl.pallas_call(partial(assemble_kernel, (len(rows), len(cols))), out_shap...  26.2 us

profile of v2, /device:TPU:0, one launch (start us, length us, event | category | flops | bytes accessed | tf_op | source)
XLA Modules:
  0.0 505.9 jit_solution(9620793073545162013)
XLA Ops:
  0.7 0.7 stack.47.order_ref
  1.3 0.8 add_select_fusion
  2.2 0.3 reduce-window.9
  2.5 0.1 slice.51
  2.6 0.1 slice_reduce_fusion
  2.7 0.1 fusion.5
  2.8 0.1 fusion.10
  2.9 0.1 dynamic_slice.51
  3.0 0.7 fusion.6
  3.7 0.1 dynamic_slice.50
  3.8 0.1 dynamic_slice.49
  3.9 0.1 dynamic_slice.48
  3.9 0.6 pad_add_fusion.1.tcol.refs_25_
  4.6 0.9 copy.29.trow.refs_24_
  5.4 1.0 fusion.3
  6.4 1.0 pad_maximum_fusion.1
  7.4 126.4 %front.1 = (bf16[512,2048]{1,0:T(8,128)(2,1)}, f32[512,1024]{1,0:T(8,128)}, bf16[512,512]{1,0:T(8,128)(2,1)}, bf16[512,256]{1,0:T(8,128)(2,1)}, bf16[512,256]{1,...) custom-call(bf16[128,2048]{1,0:T(8,128)(2,1)} %bitcast.64, ...), custom_call_target="tpu_custom_call" | custom-call | tf_op jit(solution)/shard_map/front/pallas_call | solution.py:1094
  133.8 0.0 copy-start
  133.8 0.0 copy-start.1
  133.9 0.0 slice-start
  133.9 5.9 %fusion.1 = f32[512,3072]{1,0:T(8,128)S(1)} fusion(bf16[1024,3072]{1,0:T(8,128)(2,1)} %bitcast.62, bf16[512,2048]{1,0:T(8,128)(2,1)} %get-tuple-element.55.refs_14_), kind=kOutput, calls=%fused_computation.7 | convolution fusion | flops 3221225472 | bytes 13631488 | tf_op jit(solution)/shard_map/dot_general | solution.py:27
  139.8 0.0 copy-done
  139.8 0.0 copy-done.1
  139.8 0.0 slice-start.1
  139.9 0.0 copy-start.2
  139.9 3.5 convolution_add_fusion
  143.4 0.0 slice-done
  143.4 0.0 slice-done.1
  143.4 0.0 copy-done.2
  143.4 5.7 %multiply_convert_fusion.1 = (bf16[512,1536]{1,0:T(8,128)(2,1)S(1)}, bf16[512,1536]{1,0:T(8,128)(2,1)S(1)}, bf16[512,1536]{1,0:T(8,128)(2,1)}) fusion(f32[512,3072]{1,0:T(8,128)S(1)} %convolution_add_fusion, bf16[512,2048]{1,0:T(8,128)(2,1)S(1)} %bitcast.67, bf16[1536,2048]{1,0:T(8,128)(2,1)S(1)} %bitcast.61), kind=kOutput, calls=%fused_computation.3 | convolution fusion | flops 3233808384 | bytes 19398656 | tf_op jit(solution)/shard_map/dot_general | solution.py:31
  149.1 2.1 pad_maximum_fusion.refs_17_
  151.2 323.6 %back.1 = (bf16[128,2048]{1,0:T(8,128)(2,1)}, f32[128,2048]{1,0:T(8,128)}, f32[40,128]{1,0:T(8,128)}, bf16[4,3,64,2048]{3,2,1,0:T(8,128)(2,1)}, bf16[4,4,64,3072...) custom-call(bf16[128,2048]{1,0:T(8,128)(2,1)} %bitcast.65, ...), custom_call_target="tpu_custom_call" | custom-call | tf_op jit(solution)/shard_map/back/pallas_call | solution.py:739
  474.9 1.3 slice_bitcast_fusion.2
  476.1 1.3 slice_bitcast_fusion
  477.5 0.0 copy-start.4
  477.5 0.0 copy-start.3
  477.5 26.2 %assemble.1 = (f32[1536,2048]{1,0:T(8,128)}, f32[512,2048]{1,0:T(8,128)}, f32[512,6144]{1,0:T(8,128)}, f32[512,6144]{1,0:T(8,128)}, f32[512,2048]{1,0:T(8,128)},...) custom-call(s32[5]{0:T(128)} %stack.47.order_ref, bf16[4,3,64,2048]{3,2,1,0:T(8,128)(2,1)} %get-tuple-element.60.refs_0_, ...), custom_call_target="tpu_custom_call" | custom-call | bytes 75497472 | tf_op jit(solution)/shard_map/assemble/pallas_call | solution.py:187
  503.7 0.0 copy-done.4
  503.7 0.8 copy.33
  504.5 0.0 copy-done.3
  504.5 1.0 copy.34
  (11 shorter events, 0.1 us)
Async XLA Ops:
  133.8 6.0 %copy-start = (bf16[4,4,64,3072]{3,2,1,0:T(8,128)(2,1)S(1)}, bf16[4,4,64,3072]{3,2,1,0:T(8,128)(2,1)}, u32[]{:S(2)}) copy-start(bf16[4,4,64,3072]{3,2,1,0:T(8,128)(2,1)} %get-tuple-element.48.refs_7_) | copy-start | bytes 18874372
  133.8 6.0 %copy-start.1 = (bf16[512,2048]{1,0:T(8,128)(2,1)S(1)}, bf16[512,2048]{1,0:T(8,128)(2,1)}, u32[]{:S(2)}) copy-start(bf16[512,2048]{1,0:T(8,128)(2,1)} %get-tuple-element.55.refs_14_) | copy-start | bytes 6291460
  133.9 9.5 %slice-start = ((s8[6291456]{0:T(1024)(128)(4,1)}), s8[4194304]{0:T(1024)(128)(4,1)S(1)}, s32[]{:S(2)}) async-start(s8[6291456]{0:T(1024)(128)(4,1)} %bitcast.60), calls=%async_computation | async-start | bytes 8388608
  139.8 3.5 slice-start.1
  139.9 3.5 copy-start.2
  477.5 26.2 %copy-start.4 = (bf16[128,2048]{1,0:T(8,128)(2,1)S(1)}, bf16[128,2048]{1,0:T(8,128)(2,1)}, u32[]{:S(2)}) copy-start(bf16[128,2048]{1,0:T(8,128)(2,1)} %get-tuple-element.57) | copy-start | bytes 1572868
  477.5 27.0 %copy-start.3 = (f32[128,2048]{1,0:T(8,128)S(1)}, f32[128,2048]{1,0:T(8,128)}, u32[]{:S(2)}) copy-start(f32[128,2048]{1,0:T(8,128)} %get-tuple-element.58) | copy-start | bytes 3145732
